TPU v7x, 128 devices: a whole 4x4x4 slice. The times are simulated.
128 devices in a mesh: dp: 16 (over z, y), tp: 8 (over x, core).
Axes of the slice: x: 4, y: 4, z: 4, core: 2. Of those that a mesh axis runs over, the one named last changes fastest.
Arguments:
- hidden: bfloat16 [1024, 640], P('dp')
- w_final: float32 [640], replicated
- emb_table: bfloat16 [262144, 640], P('tp')
- teacher: bfloat16 [1024, 262144], P('dp', 'tp')
- tok_mask: float32 [1024], P('dp')
Outputs:
- output 1: float32 [], replicated
- output 2: bfloat16 [1024, 640], P('dp')
- output 3: float32 [640], replicated
- output 4: float32 [262144, 640], P('tp')
All inputs are finite; a program needn't handle non-finite values.
Results may differ from a plain program's by a relative error of at most 0.001.
Values sent between devices are 32-bit elements.
A program may use at most 1 GiB of HBM per device.

v0:
```python
import jax
import jax.numpy as jnp
from jax import lax
from jax.experimental import pallas as pl
from jax.experimental.pallas import tpu as pltpu
from jax.sharding import PartitionSpec as P


SOFT_CAP = 30.0
INV_CAP = 1.0 / SOFT_CAP
NORM_EPS = 1e-6
SIDE, N_DP, N_TP, LANES = 4, 16, 8, 128
UP, DOWN, AWAY = 1, 3, 2
TILT = 8
LAST = 64
MIB = 2 ** 20
L_FRONT = 41
MESH = pl.DeviceIdType.MESH
VM = pl.BlockSpec(memory_space=pltpu.VMEM)
HB = pl.BlockSpec(memory_space=pltpu.HBM)
F32, BF16 = jnp.float32, jnp.bfloat16
ROWS_BY_ROWS = (((1,), (1,)), ((), ()))
COLS_BY_COLS = (((0,), (0,)), ((), ()))

OFFSETS = tuple((dz, dy) for dz in range(SIDE) for dy in range(SIDE))
ORDER = tuple(sorted(OFFSETS, key=lambda o: -sum(min(d, SIDE - d) for d in o)))


def shift(dp, dz, dy):
    return (dp // SIDE + dz + SIDE) % SIDE * SIDE + (dp % SIDE + dy + SIDE) % SIDE


def peers():
    me = lax.axis_index('dp')
    z, y = lax.div(me, SIDE), lax.rem(me, SIDE)
    zs = [lax.rem(z + d, SIDE) * SIDE for d in range(SIDE)]
    ys = [lax.rem(y + d, SIDE) for d in range(SIDE)]
    return me, {(dz, dy): zs[dz] + ys[dy] for dz in range(-DOWN, SIDE) for dy in range(-DOWN, SIDE)}


def aligned(start, size, unit=LANES):
    return pl.ds(pl.multiple_of(start, unit), size)


def hops(kind, dz, dy):
    along_z = [(dz, 0)] if dz % 2 else [(UP if dy < AWAY else DOWN, 0)] * dz
    along_y = [(0, dy)] if dy % 2 else [(0, UP if dz < AWAY else DOWN)] * dy
    return along_y + along_z if kind else along_z + along_y


JOBS = tuple((kind, o) for o in ORDER[:-1] for kind in range(2))
PATHS = tuple(hops(kind, *o) for kind, o in JOBS)
MIDDLE = tuple((j, level) for level in range(SIDE) for j, path in enumerate(PATHS) if len(path) > level + 1)


def waves(j, level):
    return (None,) if (j, level) in MIDDLE and level < 2 else (0, 1)


def grad_block(at, tea_ref, x_ref, tab_rows, coef_ref, z_buf, g_buf, out_ref, block):
    tokens = tea_ref.shape[1]
    span = tab_rows.shape[0]
    few = LANES // N_DP
    cols = aligned(block * span, span)
    z_buf[:, :span] = lax.dot_general(x_ref[...], tab_rows, ROWS_BY_ROWS, preferred_element_type=F32)
    for k, (dz, dy) in enumerate(OFFSETS):
        here = aligned(at[-dz, -dy] * tokens, tokens, tokens)
        ratio = jnp.tanh(z_buf[here, :span] * INV_CAP)
        stu = jnp.exp(SOFT_CAP * ratio - SOFT_CAP)
        inv_s, inv_t, _, weight = (coef_ref[0:tokens, k * few + i:k * few + i + 1] for i in range(SIDE))
        diff = (stu * inv_s - tea_ref[k, :, cols] * inv_t) * weight
        g_buf[here, :span] = (diff * (1.0 - ratio * ratio)).astype(BF16)
    out_ref[block] = lax.dot_general(g_buf[:, :span], x_ref[...], COLS_BY_COLS, preferred_element_type=F32)


def front(hidden, gain_row, mask_row, teacher, table):
    tokens, vocab = teacher.shape
    dim = hidden.shape[1]
    part = vocab // N_DP
    half = tokens // 2
    few = tokens // N_TP
    pack = 16
    sub = 512
    per = part // sub
    tiles = vocab // sub
    depth = 2 * per
    ring = N_DP // 2
    few_first = 3

    def kern(hid_hbm, gain_hbm, mask_hbm, tea_ref, tab_ref, got_late, blocks_ref, x_out, tab_out, coef_ref, all_ref, gh_ref, gg_ref,
             hid_ref, gain_ref, mask_in, w_ref, raw, sends, stage, got_soon, g_buf, t_acc, c_acc, tabs, n_buf, x_buf, inv_buf, square, pay, pay_got, mask_own, mask_got, x_got, tp_got, own_col,
             own_row, rel, dx, rs_got, ag_own, ag_got, gn_own, gn_got, raw_sem, tab_sem, in_sem, hop_out, hop_in, dp_sem, tp_sem):
        me, at = peers()
        col = lax.axis_index('tp')
        mates = [lax.rem(col + j, N_TP) for j in range(N_TP)]
        my_few = aligned(col * few, few, few)

        def fetch(k):
            d = at[ORDER[k]]
            return pltpu.make_async_copy(tea_ref.at[:, aligned(d * part, part)], raw.at[pl.ds(k % ring * tokens, tokens)], raw_sem.at[k % ring])

        def tab_copy(i):
            slot = lax.rem(i, depth)
            return pltpu.make_async_copy(tab_ref.at[aligned(lax.rem(i, tiles) * sub, sub)], tabs.at[slot], tab_sem.at[slot])

        inputs = [pltpu.make_async_copy(src, dst, in_sem.at[2 + i])
                  for i, (src, dst) in enumerate(((hid_hbm, hid_ref), (gain_hbm, gain_ref), (mask_hbm, mask_in)))]
        own_tab = pltpu.make_async_copy(tab_ref.at[aligned(me * part, part)], tab_out, in_sem.at[1])
        for cp in inputs:
            cp.start()
        for k in range(ring):
            fetch(k).start()
        for i in range(per):
            tab_copy(i).start()
        own_tab.start()
        barrier = pltpu.get_barrier_semaphore()
        for dz, dy in ORDER[:-1]:
            pl.semaphore_signal(barrier, inc=1, device_id=(at[dz, dy], col), device_id_type=MESH)
        for j in range(1, N_TP):
            pl.semaphore_signal(barrier, inc=1, device_id=(me, mates[j]), device_id_type=MESH)

        def fold(v):
            total = v[:, :LANES]
            for c in range(LANES, v.shape[1], LANES):
                total = total + v[:, c:c + LANES]
            return total

        def weigh(k):
            fetch(k).wait()
            d = at[ORDER[k]]

            def rows(r, _):
                here = aligned(r * pack, pack, pack)
                cap = jnp.tanh(raw[aligned(k % ring * tokens + r * pack, pack, pack)].astype(F32) * INV_CAP)
                tea = jnp.exp(SOFT_CAP * cap - SOFT_CAP)
                sends[aligned(d * tokens + r * pack, pack, pack)] = tea
                t_acc[here] += fold(tea)
                c_acc[here] += fold(tea * cap)
                return 0

            lax.fori_loop(0, tokens // pack, rows, 0)
            if k + ring < N_DP:
                fetch(k + ring).start()

        t_acc[...] = jnp.zeros((tokens, LANES), F32)
        c_acc[...] = jnp.zeros((tokens, LANES), F32)
        weigh(0)
        pl.semaphore_wait(barrier, N_DP + N_TP - 2)

        def remote(src, dst, out, into, dp, tp):
            return pltpu.make_async_remote_copy(src_ref=src, dst_ref=dst, send_sem=out, recv_sem=into, device_id=(dp, tp), device_id_type=MESH)

        def whole(ref, sem):
            pltpu.make_async_copy(ref, ref, sem).wait()

        def to_dp(src, dst, x, rows=slice(None)):
            for o in ORDER[:-1]:
                remote(src.at[rows], dst.at[me, rows], dp_sem.at[x, 0], dp_sem.at[x, 1], at[o], col).start()
            others = dst.at[pl.ds(0, N_DP - 1), rows]
            return [(others, dp_sem.at[x, 0])], lambda: whole(others, dp_sem.at[x, 1])

        def to_tp(srcs, dst, x):
            for c in mates[1:]:
                remote(srcs(c), dst.at[col], tp_sem.at[x, 0], tp_sem.at[x, 1], me, c).start()
            others = dst.at[pl.ds(0, N_TP - 1)]
            return [(others, tp_sem.at[x, 0])], lambda: whole(others, tp_sem.at[x, 1])

        def added(ref, here=slice(None)):
            total = ref[0, here]
            for d in range(1, ref.shape[0]):
                total = total + ref[d, here]
            return total

        gots = (got_soon, got_late)
        late = part // 2

        def hop(j, level, w):
            kind, (dz, dy) = JOBS[j]
            tok = pl.ds(kind * half, half)
            rows = slice(None) if w is None else pl.ds(w * late, late)
            src = stage.at[MIDDLE.index((j, level - 1)), :, rows] if level else sends.at[aligned(at[dz, dy] * tokens + kind * half, half, half), rows]
            dst = stage.at[MIDDLE.index((j, level)), :, rows] if (j, level) in MIDDLE else gots[w].at[dz * SIDE + dy, tok]
            into = (level if w is None else level + w) if (j, level) in MIDDLE else SIDE + w
            return remote(src, dst, hop_out.at[min(level, 1)], hop_in.at[into], at[PATHS[j][level]], col)

        def came(level, w=None):
            n = sum(at == level for _, at in MIDDLE)
            rows = slice(None) if w is None else pl.ds(0, late)
            whole(stage.at[pl.ds(0, n), :, rows], hop_in.at[level + (w or 0)])

        def onward(level, far, *ws):
            for w in ws:
                for j, at in MIDDLE:
                    if at == level - 1 and far == (len(PATHS[j]) > 2):
                        hop(j, level, w).start()

        def issue(k):
            for j, (_, to) in enumerate(JOBS):
                if to == ORDER[k]:
                    for w in waves(j, 0):
                        hop(j, 0, w).start()

        issue(0)
        for k in range(1, few_first):
            weigh(k)
            issue(k)
        for cp in inputs:
            cp.wait()
        w_ref[...] = 1.0 + jnp.concatenate([gain_ref[i:i + 1] for i in range(dim // LANES)], axis=1)
        hid = hid_ref[...].astype(F32)
        inv = lax.rsqrt(jnp.mean(hid * hid, axis=1, keepdims=True) + NORM_EPS)
        n_buf[...] = hid * inv
        x_buf[...] = (n_buf[...] * w_ref[...]).astype(BF16)
        inv_buf[...] = jnp.broadcast_to(inv, (tokens, LANES))
        pay[...] = n_buf[my_few]
        square[...] = jnp.zeros((LANES, LANES), F32)
        square[0:1, 0:tokens] = mask_in[...]
        mask_own[...] = square[0:few]
        mask_col = jnp.transpose(square[...])[0:tokens, 0:1]
        pay_sent, pay_came = to_dp(pay, pay_got, 0)
        pay_got[me] = pay[...]
        mask_sent, mask_came = to_dp(mask_own, mask_got, 1, pl.ds(0, 1))
        mask_got[me] = mask_own[...]
        for k in range(few_first, N_DP):
            weigh(k)
            issue(k)

        def keep(r, _):
            here, there = aligned(me * tokens + r * pack, pack, pack), aligned(r * pack, pack, pack)
            got_soon[0, there] = sends[here, :late]
            got_late[0, there] = sends[here, late:]
            return 0

        lax.fori_loop(0, tokens // pack, keep, 0)

        def student(slot):
            z = lax.dot_general(x_buf[...], tabs[slot], ROWS_BY_ROWS, preferred_element_type=F32)
            ratio = jnp.tanh(z * INV_CAP)
            return ratio, jnp.exp(SOFT_CAP * ratio - SOFT_CAP)

        def next_tiles(i):
            for c in range(per):
                tab_copy(i * per + c).wait()

            @pl.when(i + 1 < 2 * N_DP)
            def _():
                for c in range(per):
                    tab_copy((i + 1) * per + c).start()

            return [lax.rem(i, 2) * per + c for c in range(per)]

        def forward(i, sums):
            s_sum, k_sum = sums
            slots = next_tiles(i)
            for c in range(per):
                ratio, stu = student(slots[c])
                tea = sends[aligned(i * tokens, tokens, tokens), pl.ds(c * sub, sub)]
                s_sum, k_sum = s_sum + fold(stu), k_sum + fold(tea * ratio)
            return s_sum, k_sum

        zero = jnp.zeros((tokens, LANES), F32)
        s_sum, k_sum = lax.fori_loop(0, N_DP, forward, (zero, zero))
        lane = lax.broadcasted_iota(jnp.int32, (tokens, LANES), 1)
        sums = jnp.where(lane == 0, jnp.sum(s_sum, axis=1, keepdims=True), 0.0)
        sums = jnp.where(lane == 1, jnp.sum(t_acc[...], axis=1, keepdims=True), sums)
        sums = jnp.where(lane == AWAY, SOFT_CAP * jnp.sum(c_acc[...] - k_sum, axis=1, keepdims=True), sums)
        own_col[...] = sums
        tp_got[col] = sums
        tp_sent, tp_came = to_tp(lambda c: own_col, tp_got, 0)
        tp_came()
        total = added(tp_got)
        square[0:tokens] = jnp.where(lane == DOWN, mask_col, total)
        line = jnp.transpose(square[...])[0:few]
        own_row[...] = line
        all_ref[me] = line
        dp_sent, dp_came = to_dp(own_row, all_ref, 2)
        twin = col + 1 - 2 * lax.rem(col, 2)
        pay_came()
        mask_came()
        x_got[col] = pay_got[...]

        evens = range(0, N_TP, 2)
        for j in evens[1:]:
            remote(pay_got, x_got.at[col], tp_sem.at[1, 0], tp_sem.at[1, 1], me, mates[j]).start()
        came(0)
        onward(1, True, None)
        onward(1, False, 0)

        count = jnp.sum(added(mask_got, slice(1)), axis=1, keepdims=True)
        inv_s, inv_t, weight = 1.0 / total[:, 0:1], 1.0 / total[:, 1:2], mask_col / count
        dx[...] = jnp.zeros((tokens, dim), F32)

        def backward(i, _):
            slots = next_tiles(i)
            total = dx[...]
            for c in range(per):
                ratio, stu = student(slots[c])
                tea = sends[aligned((i - N_DP) * tokens, tokens, tokens), pl.ds(c * sub, sub)]
                diff = (stu * inv_s - tea * inv_t) * weight
                g = (diff * (1.0 - ratio * ratio)).astype(BF16)
                total = total + jnp.dot(g, tabs[slots[c]], preferred_element_type=F32)
            dx[...] = total
            return 0

        lax.fori_loop(N_DP, 2 * N_DP, backward, 0)
        came(1)
        onward(2, True, 0)
        onward(1, False, 1)
        whole(x_got.at[pl.ds(0, SIDE - 1)], tp_sem.at[1, 1])
        for j in evens:
            remote(x_got.at[mates[j]], x_got.at[mates[j]], tp_sem.at[SIDE, 0], tp_sem.at[SIDE, 1], me, twin).start()

        rs_got[col] = dx[my_few]
        rs_sent, rs_came = to_tp(lambda c: dx.at[aligned(c * few, few, few)], rs_got, 2)
        rs_came()
        my_x = added(rs_got)
        my_n = n_buf[my_few]
        grad_n = my_x * w_ref[...]
        my_h = inv_buf[my_few, 0:1] * (grad_n - my_n * jnp.mean(grad_n * my_n, axis=1, keepdims=True))
        ag_own[...] = jnp.zeros((2 * few, dim), F32)
        ag_own[0:few] = my_h
        ag_own[few:few + 1] = jnp.sum(my_x * my_n, axis=0, keepdims=True)
        ag_got[col] = ag_own[...]
        ag_sent, ag_came = to_tp(lambda c: ag_own, ag_got, DOWN)
        ag_came()
        gh_ref[...] = jnp.concatenate([ag_got[j, 0:few] for j in range(N_TP)], axis=0)
        line = added(ag_got, slice(few, few + 1))
        gn_own[0:1] = line
        gn_got[me, 0:1] = line
        gn_sent, gn_came = to_dp(gn_own, gn_got, DOWN, pl.ds(0, 1))

        came(2, 0)
        onward(DOWN, True, 0)
        onward(2, True, 1)
        whole(x_got.at[pl.ds(0, SIDE)], tp_sem.at[SIDE, 1])

        def widen(d, _):
            rows = jnp.concatenate([x_got[j, d] for j in range(N_TP)], axis=0)
            x_out[aligned(d * tokens, tokens, tokens)] = (rows * w_ref[...]).astype(BF16)
            return 0

        lax.fori_loop(0, N_DP, widen, 0)
        dp_came()
        row = lax.broadcasted_iota(jnp.int32, (few, LANES), 0)
        lanes = lax.broadcasted_iota(jnp.int32, (few, LANES), 1)
        for d in range(N_DP):
            block = all_ref[d]
            safe = jnp.where((row < AWAY) & (lanes < tokens), block, 1.0)
            rel[d * few:(d + 1) * few] = jnp.where(row < AWAY, 1.0 / safe, block / count)
        for k, (dz, dy) in enumerate(OFFSETS):
            square[k * few:(k + 1) * few] = rel[aligned(at[-dz, -dy] * few, few, few)]
        coef_ref[...] = jnp.transpose(square[...])

        own_tab.wait()
        whole(got_soon.at[pl.ds(0, N_DP - 1)], hop_in.at[SIDE])
        whole(sends.at[pl.ds(0, len(JOBS) * half)], hop_out.at[0])

        def block(b, _):
            @pl.when(b == 1)
            def _():
                came(2, 1)
                onward(DOWN, True, 1)

            grad_block(at, got_soon, x_out, tab_out[aligned(b * sub, sub)], coef_ref, sends, g_buf, blocks_ref, b)
            return 0

        lax.fori_loop(0, 2, block, 0)
        gn_came()
        gg_ref[...] = added(gn_got, slice(1))
        whole(got_late.at[pl.ds(0, N_DP - 1)], hop_in.at[SIDE + 1])
        whole(stage, hop_out.at[1])
        for ref, sem in (*pay_sent, *mask_sent, *tp_sent, *dp_sent, *rs_sent, *ag_sent, *gn_sent):
            whole(ref, sem)
        whole(x_got.at[pl.ds(0, SIDE - 1)], tp_sem.at[1, 0])
        whole(x_got.at[pl.ds(0, SIDE)], tp_sem.at[SIDE, 0])

    dma = pltpu.SemaphoreType.DMA
    wide, flat = (tokens, dim), (few, LANES)
    return pl.pallas_call(
        kern,
        out_shape=tuple(jax.ShapeDtypeStruct(shape, kind) for shape, kind in (
            ((N_DP, tokens, part // 2), F32), ((2, sub, dim), F32), ((N_DP * tokens, dim), BF16), ((part, dim), BF16), ((LANES, LANES), F32), ((N_DP, *flat), F32), (wide, F32),
            ((1, dim), F32))),
        in_specs=[HB] * 5, out_specs=(VM,) * 8,
        scratch_shapes=[pltpu.VMEM(shape, kind) for shape, kind in (
            (wide, BF16), ((dim // LANES, LANES), F32), ((1, tokens), F32), ((1, dim), F32), ((ring * tokens, part), BF16), ((N_DP * tokens, part), F32),
            ((len(MIDDLE), half, part), F32), ((N_DP, tokens, part // 2), F32), ((N_DP * tokens, sub), BF16), ((tokens, LANES), F32), ((tokens, LANES), F32),
            ((depth, sub, dim), BF16), (wide, F32), (wide, BF16), ((tokens, LANES), F32), ((LANES, LANES), F32), ((few, dim), F32),
            ((N_DP, few, dim), F32), (flat, F32), ((N_DP, *flat), F32), ((N_TP, N_DP, few, dim), F32), ((N_TP, tokens, LANES), F32),
            ((tokens, LANES), F32), (flat, F32), ((LANES, LANES), F32), (wide, F32), ((N_TP, few, dim), F32), ((2 * few, dim), F32),
            ((N_TP, 2 * few, dim), F32), ((few, dim), F32), ((N_DP, few, dim), F32))] + [
            dma((ring,)), dma((depth,)), dma((5,)), dma((2,)), dma((SIDE + 2,)), dma((SIDE, 2)), dma((SIDE + 1, 2))],
        compiler_params=pltpu.CompilerParams(collective_id=0, has_side_effects=True, vmem_limit_bytes=L_FRONT * MIB),
        cost_estimate=pl.CostEstimate(flops=3 * 10 ** 9, bytes_accessed=100 * MIB, transcendentals=0), name='front')(
            *(pltpu.with_memory_space_constraint(a, pltpu.HBM) for a in (hidden, gain_row, mask_row, teacher, table)))


def finish(teas, x_all, tab_part, coef):
    n, tokens, late = teas.shape
    dim = x_all.shape[1]
    span = late // 2

    def kern(tea_ref, x_ref, tab_ref, coef_ref, out_ref, z_buf, g_buf):
        at = peers()[1]

        def block(b, _):
            grad_block(at, tea_ref, x_ref, tab_ref[aligned(late + b * span, span)], coef_ref, z_buf, g_buf, out_ref, b)
            return 0

        lax.fori_loop(0, 2, block, 0)

    return pl.pallas_call(kern, out_shape=jax.ShapeDtypeStruct((2, span, dim), F32), in_specs=[VM] * 4, out_specs=VM,
        scratch_shapes=[pltpu.VMEM((n * tokens, span), F32), pltpu.VMEM((n * tokens, span), BF16)], name='finish',
        compiler_params=pltpu.CompilerParams(vmem_limit_bytes=22 * MIB),
        cost_estimate=pl.CostEstimate(flops=10 ** 9, bytes_accessed=8 * MIB, transcendentals=0))(teas, x_all, tab_part, coef)


def place(table, pieces, vocab):
    arrays = [p[0] for p in pieces]
    n = len(arrays)
    dim = arrays[0].shape[1]
    rows = vocab // N_DP
    quarter = rows // SIDE
    cut = 256
    chunks = []
    for i, (array, dz, dy, kind, start) in enumerate(pieces):
        r = 0
        while r < array.shape[0]:
            row = start + r
            size = min(cut, array.shape[0] - r, quarter - row % quarter)
            chunks.append((i, r, size, dz, dy, row + (row // quarter + kind) * quarter))
            r += size

    def kern(*refs):
        dst, buf, sem = refs[-DOWN:]
        at = peers()[1]
        reads, writes = [], []
        for k, (i, r, size, dz, dy, first) in enumerate(chunks):
            held = buf.at[k, pl.ds(0, size)]
            there = aligned(at[dz, dy] * rows + first, size, 8)
            reads.append(pltpu.make_async_copy(refs[i].at[pl.ds(r, size)], held, sem.at[0, k]))
            writes.append(pltpu.make_async_copy(held, dst.at[there], sem.at[1, k]))
        for cp in reads:
            cp.start()
        for read, write in zip(reads, writes):
            read.wait()
            write.start()
        for cp in writes:
            cp.wait()

    args = arrays if table is None else [*arrays, table]
    size = len(chunks) * cut * dim
    return pl.pallas_call(kern, out_shape=jax.ShapeDtypeStruct((vocab, dim), F32), in_specs=[pl.BlockSpec(memory_space=pl.ANY)] * n + [HB] * (len(args) - n),
        out_specs=HB, scratch_shapes=[pltpu.VMEM((len(chunks), cut, dim), F32), pltpu.SemaphoreType.DMA((2, len(chunks)))],
        input_output_aliases={} if table is None else {n: 0}, name='place', compiler_params=pltpu.CompilerParams(vmem_limit_bytes=4 * size + MIB),
        cost_estimate=pl.CostEstimate(flops=10 * MIB, bytes_accessed=8 * size, transcendentals=0))(*args)


def gather(first, rest, vocab):
    quarter = first[0].shape[0]
    sets, ways = range(2), (UP, DOWN)
    table, event = None, 0

    def send(pair, axis, step):
        out = []
        for k in sets:
            dz, dy = (step, 0) if axis == k else (0, step)
            out.append(lax.ppermute(pair[k], 'dp', [(d, shift(d, dz, dy)) for d in range(N_DP)]))
        return out

    def put(pair, a, b, start=0):
        return [(pair[k], *((b, a) if k else (a, b)), k, start) for k in sets]

    def settle(*pieces):
        nonlocal table
        table = place(table, [p for ps in pieces for p in ps], vocab)

    def wait(*pairs):
        nonlocal table, event
        event += 1
        table, *flat = lax.optimization_barrier((table, *(x for pair in pairs for x in pair)))
        return [flat[2 * i:2 * i + 2] for i in range(len(pairs))]

    def join(one, other):
        return [jnp.concatenate(pair) for pair in zip(one, other)]

    own = [first]
    low, high = ([send(own[0], 0, way)] for way in ways)
    later = rest()
    event = 1
    own.append([later[:quarter], later[quarter:]])
    low.append(send(own[1], 0, UP))
    high.append(send(own[1], 0, DOWN))
    whole = join(*own)
    side = {way: send(whole, 1, way) for way in ways}
    settle(put(own[0], 0, 0, 0), put(own[1], 0, 0, quarter))

    low[0], high[0] = wait(low[0], high[0])
    far_low = send(low[0], 0, UP)
    settle(put(low[0], DOWN, 0, 0), put(high[0], UP, 0, 0))

    low[1], high[1] = wait(low[1], high[1])
    far_high = send(high[1], 0, DOWN)
    low_whole, high_whole = join(*low), join(*high)
    low_side = {way: send(low_whole, 1, way) for way in ways}
    settle(put(low[1], DOWN, 0, quarter), put(high[1], UP, 0, quarter))

    side[UP], side[DOWN], high_whole = wait(side[UP], side[DOWN], high_whole)
    high_side = {way: send(high_whole, 1, way) for way in ways}
    side_far = send(side[UP], 1, UP)
    settle(put(side[UP], 0, DOWN))
    settle(put(side[DOWN], 0, UP))

    far_low, far_high = wait(far_low, far_high)
    far_side = {(c, way): send(pair, 1, way) for way in ways for c, pair in enumerate((far_low, far_high))}
    settle(put(far_low, AWAY, 0, 0), put(far_high, AWAY, 0, quarter))

    low_side[UP], low_side[DOWN] = wait(low_side[UP], low_side[DOWN])
    low_far = send(low_side[DOWN], 1, DOWN)
    settle(put(low_side[UP], DOWN, DOWN))
    settle(put(low_side[DOWN], DOWN, UP))

    high_side[UP], high_side[DOWN] = wait(high_side[UP], high_side[DOWN])
    cut = quarter + TILT
    high_far = [send([x[:cut] for x in high_side[UP]], 1, UP), send([x[cut:] for x in high_side[DOWN]], 1, DOWN)]
    settle(put(high_side[UP], UP, DOWN))
    settle(put(high_side[DOWN], UP, UP))

    far_side[0, DOWN], far_side[1, DOWN], side_far = wait(far_side[0, DOWN], far_side[1, DOWN], side_far)
    ends = slice(0, quarter - LAST), slice(quarter - LAST, quarter)
    last_down = [send([x[end] for x in far_side[1, DOWN]], 1, DOWN) for end in ends]
    settle(put(far_side[0, DOWN], AWAY, UP, 0), put(far_side[1, DOWN], AWAY, UP, quarter))
    settle(put(side_far, 0, AWAY))

    far_side[0, UP], = wait(far_side[0, UP])
    last_up = [send([x[end] for x in far_side[0, UP]], 1, UP) for end in ends]
    settle(put(far_side[0, UP], AWAY, DOWN, 0))

    far_side[1, UP], low_far = wait(far_side[1, UP], low_far)
    settle(put(far_side[1, UP], AWAY, DOWN, quarter))
    settle(put(low_far, DOWN, AWAY))

    high_far = wait(*high_far)
    settle(put(high_far[0], UP, AWAY, 0), put(high_far[1], UP, AWAY, cut))
    for up, down, end in zip(last_up, last_down, ends):
        up, down = wait(up, down)
        settle(put(up, AWAY, AWAY, end.start), put(down, AWAY, AWAY, quarter + end.start))
    return table


def solution(mesh):
    def local_step(hid_rows, w_final, tab_rows, tea_rows, mask_rows):
        tokens = hid_rows.shape[0]
        late, soon, x_all, tab_part, coef, stats, grad_h, gain_line = front(hid_rows, w_final.reshape(-1, LANES), mask_rows[None], tea_rows, tab_rows)
        coef, *first = lax.optimization_barrier((coef, soon[0], soon[1]))
        table = gather(first, lambda: finish(late, x_all, tab_part, coef).reshape(-1, x_all.shape[1]), tab_rows.shape[0])
        s_sum, t_sum, k_sum, masks = (stats[:, i, :tokens] for i in range(SIDE))
        all_kl = k_sum / t_sum + jnp.log(s_sum) - jnp.log(t_sum)
        loss_val = jnp.sum(masks * all_kl) / jnp.sum(masks)
        return loss_val, grad_h.astype(BF16), gain_line[0], table

    return jax.shard_map(local_step, mesh=mesh, in_specs=(P('dp', None), P(None), P('tp', None), P('dp', 'tp'), P('dp')), out_specs=(P(), P('dp', None), P(None), P('tp', None)), check_vma=False)
```

profile of v0, /device:TPU:0, one launch (start us, length us, event | category | flops | bytes accessed | tf_op | source)
XLA Modules:
  0.0 668.2 jit_solution(1065889254382163701)
XLA Ops:
  0.6 105.4 %front.1 = (f32[16,64,1024]{2,1,0:T(8,128)S(1)}, f32[2,512,640]{2,1,0:T(8,128)S(1)}, bf16[1024,640]{1,0:T(8,128)(2,1)S(1)}, bf16[2048,640]{1,0:T(8,128)(2,1)S(1)...) custom-call(bf16[64,640]{1,0:T(8,128)(2,1)} %hid_hbm.1, ...), custom_call_target="tpu_custom_call" | custom-call | flops 3000000000 | bytes 104857600 | tf_op jit(solution)/shard_map/front/pallas_call | solution.py:379
  108.0 3.2 collective-permute-start.2
  112.8 7.3 %finish.1 = f32[2,512,640]{2,1,0:T(8,128)S(1)} custom-call(f32[16,64,1024]{2,1,0:T(8,128)S(1)} %get-tuple-element.84.tea_ref, bf16[1024,640]{1,0:T(8,128)(2,1)S(1)} %get-tuple-element.85.x_ref, bf16[2048,640]{1,0:T(8,128)(2,1)S(1)} %get-tuple-element.86.tab_ref, f32[128,128]{1,0:T(8,128)S(1)} %get-tuple-element.87.coef_ref), custom_call_target="tpu_custom_call" | custom-call | flops 1000000000 | bytes 8388608 | tf_op jit(solution)/shard_map/finish/pallas_call | solution.py:412
  120.6 18.6 %collective-permute-done.refs_0_ = f32[512,640]{1,0:T(8,128)S(1)} collective-permute-done((f32[512,640]{1,0:T(8,128)S(1)}, f32[512,640]{1,0:T(8,128)S(1)}, u32[]{:S(2)}, u32[]{:S(2)}) %collective-permute-start) | collective-permute-done | bytes 1310752 | tf_op jit(solution)/shard_map/ppermute | solution.py:468
  144.6 22.7 %collective-permute-done.4.refs_0_ = f32[512,640]{1,0:T(8,128)S(1)} collective-permute-done((f32[512,640]{1,0:T(8,128)S(1)}, f32[512,640]{1,0:T(8,128)S(1)}, u32[]{:S(2)}, u32[]{:S(2)}) %collective-permute-start.4) | collective-permute-done | bytes 1310752 | tf_op jit(solution)/shard_map/ppermute | solution.py:468
  168.8 3.2 collective-permute-done.5.refs_1_
  174.3 4.1 place.18.refs_4_
  179.6 70.2 %collective-permute-done.7.refs_3_ = f32[512,640]{1,0:T(8,128)S(1)} collective-permute-done((f32[512,640]{1,0:T(8,128)S(1)}, f32[512,640]{1,0:T(8,128)S(1)}, u32[]{:S(2)}, u32[]{:S(2)}) %collective-permute-start.7) | collective-permute-done | bytes 1310752 | tf_op jit(solution)/shard_map/ppermute | solution.py:468
  251.9 4.1 place.19.refs_4_
  257.2 3.2 collective-permute-start.14
  262.9 19.8 %collective-permute-done.12.refs_0_ = f32[512,640]{1,0:T(8,128)} collective-permute-done((f32[512,640]{1,0:T(8,128)S(1)}, f32[512,640]{1,0:T(8,128)}, u32[]{:S(2)}, u32[]{:S(2)}) %collective-permute-start.12) | collective-permute-done | bytes 1310752 | tf_op jit(solution)/shard_map/ppermute | solution.py:468
  282.7 3.7 collective-permute-start.18
  286.4 3.1 collective-permute-done.14.refs_2_
  289.6 2.8 collective-permute-start.15
  292.3 4.1 place.20.refs_2_
  296.8 63.8 %collective-permute-done.15.refs_3_ = f32[512,640]{1,0:T(8,128)} collective-permute-done((f32[512,640]{1,0:T(8,128)S(1)}, f32[512,640]{1,0:T(8,128)}, u32[]{:S(2)}, u32[]{:S(2)}) %collective-permute-start.15) | collective-permute-done | bytes 1310752 | tf_op jit(solution)/shard_map/ppermute | solution.py:468
  360.6 4.6 place.21.refs_2_
  365.2 4.1 place.22.refs_4_
  369.4 3.9 collective-permute-start.24
  373.3 2.1 collective-permute-start.26
  375.4 27.4 %collective-permute-done.24.refs_0_ = f32[512,640]{1,0:T(8,128)S(1)} collective-permute-done((f32[512,640]{1,0:T(8,128)}, f32[512,640]{1,0:T(8,128)S(1)}, u32[]{:S(2)}, u32[]{:S(2)}) %collective-permute-start.24) | collective-permute-done | bytes 1310752 | tf_op jit(solution)/shard_map/ppermute | solution.py:468
  406.2 2.3 collective-permute-start.22
  408.5 22.3 %collective-permute-done.26.refs_2_ = f32[512,640]{1,0:T(8,128)S(1)} collective-permute-done((f32[512,640]{1,0:T(8,128)}, f32[512,640]{1,0:T(8,128)S(1)}, u32[]{:S(2)}, u32[]{:S(2)}) %collective-permute-start.26) | collective-permute-done | bytes 1310752 | tf_op jit(solution)/shard_map/ppermute | solution.py:468
  436.8 27.9 %collective-permute-done.21.refs_1_ = f32[1024,640]{1,0:T(8,128)S(1)} collective-permute-done((f32[1024,640]{1,0:T(8,128)S(1)}, f32[1024,640]{1,0:T(8,128)S(1)}, u32[]{:S(2)}, u32[]{:S(2)}) %collective-permute-start.21) | collective-permute-done | bytes 2621472 | tf_op jit(solution)/shard_map/ppermute | solution.py:468
  466.6 8.0 %collective-permute-done.22.refs_0_ = f32[1024,640]{1,0:T(8,128)S(1)} collective-permute-done((f32[1024,640]{1,0:T(8,128)S(1)}, f32[1024,640]{1,0:T(8,128)S(1)}, u32[]{:S(2)}, u32[]{:S(2)}) %collective-permute-start.22) | collective-permute-done | bytes 2621472 | tf_op jit(solution)/shard_map/ppermute | solution.py:468
  479.6 14.7 %collective-permute-done.28.refs_0_ = f32[1024,640]{1,0:T(8,128)S(1)} collective-permute-done((f32[1024,640]{1,0:T(8,128)S(1)}, f32[1024,640]{1,0:T(8,128)S(1)}, u32[]{:S(2)}, u32[]{:S(2)}) %collective-permute-start.28) | collective-permute-done | bytes 2621472 | tf_op jit(solution)/shard_map/ppermute | solution.py:468
  497.9 4.6 place.23.refs_2_
  502.6 4.1 place.24.refs_2_
  506.7 4.1 place.25.refs_2_
  510.9 4.1 place.26.refs_2_
  515.1 4.1 place.27.refs_4_
  521.0 4.1 place.28.refs_2_
  525.2 4.7 place.29.refs_2_
  529.9 19.2 %collective-permute-done.31.refs_1_ = f32[512,640]{1,0:T(8,128)} collective-permute-done((f32[512,640]{1,0:T(8,128)}, f32[512,640]{1,0:T(8,128)}, u32[]{:S(2)}, u32[]{:S(2)}) %collective-permute-start.31) | collective-permute-done | bytes 1310752 | tf_op jit(solution)/shard_map/ppermute | solution.py:468
  555.7 3.2 collective-permute-start.35
  558.9 5.2 collective-permute-done.33.refs_1_
  564.2 3.6 collective-permute-start.38
  568.1 2.5 collective-permute-start.42
  570.7 12.4 %collective-permute-done.41.refs_1_ = f32[448,640]{1,0:T(8,128)S(1)} collective-permute-done((f32[448,640]{1,0:T(8,128)S(1)}, f32[448,640]{1,0:T(8,128)S(1)}, u32[]{:S(2)}, u32[]{:S(2)}) %collective-permute-start.41) | collective-permute-done | bytes 1146912 | tf_op jit(solution)/shard_map/ppermute | solution.py:468
  584.1 32.0 %collective-permute-done.42.refs_2_ = f32[448,640]{1,0:T(8,128)S(1)} collective-permute-done((f32[448,640]{1,0:T(8,128)S(1)}, f32[448,640]{1,0:T(8,128)S(1)}, u32[]{:S(2)}, u32[]{:S(2)}) %collective-permute-start.42) | collective-permute-done | bytes 1146912 | tf_op jit(solution)/shard_map/ppermute | solution.py:468
  618.8 3.5 collective-permute-start.37
  633.4 2.8 collective-permute-done.36.refs_0_
  640.0 3.0 collective-permute-start.47
  646.2 2.6 place.30.refs_2_
  648.9 2.8 place.31.refs_2_
  652.2 4.1 place.32.refs_4_
  656.4 4.2 place.33.refs_4_
  660.6 4.5 place.34.refs_4_
  (152 shorter events, 72.1 us)
Async XLA Ops:
  106.2 32.9 %collective-permute-start = (f32[512,640]{1,0:T(8,128)S(1)}, f32[512,640]{1,0:T(8,128)S(1)}, u32[]{:S(2)}, u32[]{:S(2)}) collective-permute-start(f32[512,640]{1,0:T(8,128)S(1)} %get-tuple-element.82.refs_0_), channel_id=1, source_target_pairs={{0,32},{8,40},{16,48},{24,56},{32,64},{40,72},{48,80},{56,88},{64,... | collective-permute-start | bytes 3932168 | tf_op jit(solution)/shard_map/ppermute | solution.py:468
  107.5 33.2 %collective-permute-start.1 = (f32[512,640]{1,0:T(8,128)S(1)}, f32[512,640]{1,0:T(8,128)S(1)}, u32[]{:S(2)}, u32[]{:S(2)}) collective-permute-start(f32[512,640]{1,0:T(8,128)S(1)} %get-tuple-element.83.refs_1_), channel_id=1, source_target_pairs={{0,8},{8,16},{16,24},{24,0},{32,40},{40,48},{48,56},{56,32},{64,72... | collective-permute-start | bytes 3932168 | tf_op jit(solution)/shard_map/ppermute | solution.py:468
  108.0 33.4 %collective-permute-start.2 = (f32[512,640]{1,0:T(8,128)S(1)}, f32[512,640]{1,0:T(8,128)S(1)}, u32[]{:S(2)}, u32[]{:S(2)}) collective-permute-start(f32[512,640]{1,0:T(8,128)S(1)} %get-tuple-element.82.refs_0_), channel_id=1, source_target_pairs={{0,96},{8,104},{16,112},{24,120},{32,0},{40,8},{48,16},{56,24},{64... | collective-permute-start | bytes 3932168 | tf_op jit(solution)/shard_map/ppermute | solution.py:468
  111.1 32.1 %collective-permute-start.3 = (f32[512,640]{1,0:T(8,128)S(1)}, f32[512,640]{1,0:T(8,128)S(1)}, u32[]{:S(2)}, u32[]{:S(2)}) collective-permute-start(f32[512,640]{1,0:T(8,128)S(1)} %get-tuple-element.83.refs_1_), channel_id=1, source_target_pairs={{0,24},{8,0},{16,8},{24,16},{32,56},{40,32},{48,40},{56,48},{64,88... | collective-permute-start | bytes 3932168 | tf_op jit(solution)/shard_map/ppermute | solution.py:468
  120.3 47.0 %collective-permute-start.4 = (f32[512,640]{1,0:T(8,128)S(1)}, f32[512,640]{1,0:T(8,128)S(1)}, u32[]{:S(2)}, u32[]{:S(2)}) collective-permute-start(f32[512,640]{1,0:T(8,128)S(1)} %get-tuple-element.153.refs_2_), channel_id=1, source_target_pairs={{0,32},{8,40},{16,48},{24,56},{32,64},{40,72},{48,80},{56,88},{64,... | collective-permute-start | bytes 3932168 | tf_op jit(solution)/shard_map/ppermute | solution.py:468
  139.2 32.9 %collective-permute-start.5 = (f32[512,640]{1,0:T(8,128)S(1)}, f32[512,640]{1,0:T(8,128)S(1)}, u32[]{:S(2)}, u32[]{:S(2)}) collective-permute-start(f32[512,640]{1,0:T(8,128)S(1)} %get-tuple-element.152.refs_3_), channel_id=1, source_target_pairs={{0,8},{8,16},{16,24},{24,0},{32,40},{40,48},{48,56},{56,32},{64,72... | collective-permute-start | bytes 3932168 | tf_op jit(solution)/shard_map/ppermute | solution.py:468
  140.8 31.6 %collective-permute-start.6 = (f32[512,640]{1,0:T(8,128)S(1)}, f32[512,640]{1,0:T(8,128)S(1)}, u32[]{:S(2)}, u32[]{:S(2)}) collective-permute-start(f32[512,640]{1,0:T(8,128)S(1)} %get-tuple-element.153.refs_2_), channel_id=1, source_target_pairs={{0,96},{8,104},{16,112},{24,120},{32,0},{40,8},{48,16},{56,24},{64... | collective-permute-start | bytes 3932168 | tf_op jit(solution)/shard_map/ppermute | solution.py:468
  141.4 108.4 %collective-permute-start.8 = (f32[1024,640]{1,0:T(8,128)S(1)}, f32[1024,640]{1,0:T(8,128)S(1)}, u32[]{:S(2)}, u32[]{:S(2)}) collective-permute-start(f32[1024,640]{1,0:T(8,128)S(1)} %pad_maximum_fusion), channel_id=1, source_target_pairs={{0,8},{8,16},{16,24},{24,0},{32,40},{40,48},{48,56},{56,32},{64,72... | collective-permute-start | bytes 7864328 | tf_op jit(solution)/shard_map/ppermute | solution.py:468
  143.2 113.9 %collective-permute-start.9 = (f32[1024,640]{1,0:T(8,128)S(1)}, f32[1024,640]{1,0:T(8,128)}, u32[]{:S(2)}, u32[]{:S(2)}) collective-permute-start(f32[1024,640]{1,0:T(8,128)S(1)} %pad_maximum_fusion.1), channel_id=1, source_target_pairs={{0,32},{8,40},{16,48},{24,56},{32,64},{40,72},{48,80},{56,88},{64,... | collective-permute-start | bytes 7864328 | tf_op jit(solution)/shard_map/ppermute | solution.py:468
  167.3 93.1 %collective-permute-start.10 = (f32[1024,640]{1,0:T(8,128)S(1)}, f32[1024,640]{1,0:T(8,128)S(1)}, u32[]{:S(2)}, u32[]{:S(2)}) collective-permute-start(f32[1024,640]{1,0:T(8,128)S(1)} %pad_maximum_fusion), channel_id=1, source_target_pairs={{0,24},{8,0},{16,8},{24,16},{32,56},{40,32},{48,40},{56,48},{64,88... | collective-permute-start | bytes 7864328 | tf_op jit(solution)/shard_map/ppermute | solution.py:468
  172.0 90.9 %collective-permute-start.11 = (f32[1024,640]{1,0:T(8,128)S(1)}, f32[1024,640]{1,0:T(8,128)S(1)}, u32[]{:S(2)}, u32[]{:S(2)}) collective-permute-start(f32[1024,640]{1,0:T(8,128)S(1)} %pad_maximum_fusion.1), channel_id=1, source_target_pairs={{0,96},{8,104},{16,112},{24,120},{32,0},{40,8},{48,16},{56,24},{64... | collective-permute-start | bytes 7864328 | tf_op jit(solution)/shard_map/ppermute | solution.py:468
  172.4 77.4 %collective-permute-start.7 = (f32[512,640]{1,0:T(8,128)S(1)}, f32[512,640]{1,0:T(8,128)S(1)}, u32[]{:S(2)}, u32[]{:S(2)}) collective-permute-start(f32[512,640]{1,0:T(8,128)S(1)} %get-tuple-element.152.refs_3_), channel_id=1, source_target_pairs={{0,24},{8,0},{16,8},{24,16},{32,56},{40,32},{48,40},{56,48},{64,88... | collective-permute-start | bytes 3932168 | tf_op jit(solution)/shard_map/ppermute | solution.py:468
  249.8 33.0 %collective-permute-start.12 = (f32[512,640]{1,0:T(8,128)S(1)}, f32[512,640]{1,0:T(8,128)}, u32[]{:S(2)}, u32[]{:S(2)}) collective-permute-start(f32[512,640]{1,0:T(8,128)S(1)} %collective-permute-done.refs_0_), channel_id=1, source_target_pairs={{0,32},{8,40},{16,48},{24,56},{32,64},{40,72},{48,80},{56,88},{64,... | collective-permute-start | bytes 3932168 | tf_op jit(solution)/shard_map/ppermute | solution.py:468
  249.8 36.7 %collective-permute-start.13 = (f32[512,640]{1,0:T(8,128)S(1)}, f32[512,640]{1,0:T(8,128)}, u32[]{:S(2)}, u32[]{:S(2)}) collective-permute-start(f32[512,640]{1,0:T(8,128)S(1)} %collective-permute-done.1.refs_1_), channel_id=1, source_target_pairs={{0,8},{8,16},{16,24},{24,0},{32,40},{40,48},{48,56},{56,32},{64,72... | collective-permute-start | bytes 3932168 | tf_op jit(solution)/shard_map/ppermute | solution.py:468
  257.2 32.4 %collective-permute-start.14 = (f32[512,640]{1,0:T(8,128)S(1)}, f32[512,640]{1,0:T(8,128)}, u32[]{:S(2)}, u32[]{:S(2)}) collective-permute-start(f32[512,640]{1,0:T(8,128)S(1)} %collective-permute-done.6.refs_2_), channel_id=1, source_target_pairs={{0,96},{8,104},{16,112},{24,120},{32,0},{40,8},{48,16},{56,24},{64... | collective-permute-start | bytes 3932168 | tf_op jit(solution)/shard_map/ppermute | solution.py:468
  260.4 109.0 %collective-permute-start.16 = (f32[1024,640]{1,0:T(8,128)}, f32[1024,640]{1,0:T(8,128)S(1)}, u32[]{:S(2)}, u32[]{:S(2)}) collective-permute-start(f32[1024,640]{1,0:T(8,128)} %constant_dynamic-update-slice_fusion), channel_id=1, source_target_pairs={{0,8},{8,16},{16,24},{24,0},{32,40},{40,48},{48,56},{56,32},{64,72... | collective-permute-start | bytes 7864328 | tf_op jit(solution)/shard_map/ppermute | solution.py:468
  262.9 110.3 %collective-permute-start.17 = (f32[1024,640]{1,0:T(8,128)}, f32[1024,640]{1,0:T(8,128)S(1)}, u32[]{:S(2)}, u32[]{:S(2)}) collective-permute-start(f32[1024,640]{1,0:T(8,128)} %constant_dynamic-update-slice_fusion.2), channel_id=1, source_target_pairs={{0,32},{8,40},{16,48},{24,56},{32,64},{40,72},{48,80},{56,88},{64,... | collective-permute-start | bytes 7864328 | tf_op jit(solution)/shard_map/ppermute | solution.py:468
  282.7 90.5 %collective-permute-start.18 = (f32[1024,640]{1,0:T(8,128)}, f32[1024,640]{1,0:T(8,128)S(1)}, u32[]{:S(2)}, u32[]{:S(2)}) collective-permute-start(f32[1024,640]{1,0:T(8,128)} %constant_dynamic-update-slice_fusion), channel_id=1, source_target_pairs={{0,24},{8,0},{16,8},{24,16},{32,56},{40,32},{48,40},{56,48},{64,88... | collective-permute-start | bytes 7864328 | tf_op jit(solution)/shard_map/ppermute | solution.py:468
  286.4 88.9 %collective-permute-start.19 = (f32[1024,640]{1,0:T(8,128)}, f32[1024,640]{1,0:T(8,128)S(1)}, u32[]{:S(2)}, u32[]{:S(2)}) collective-permute-start(f32[1024,640]{1,0:T(8,128)} %constant_dynamic-update-slice_fusion.2), channel_id=1, source_target_pairs={{0,96},{8,104},{16,112},{24,120},{32,0},{40,8},{48,16},{56,24},{64... | collective-permute-start | bytes 7864328 | tf_op jit(solution)/shard_map/ppermute | solution.py:468
  289.6 71.0 %collective-permute-start.15 = (f32[512,640]{1,0:T(8,128)S(1)}, f32[512,640]{1,0:T(8,128)}, u32[]{:S(2)}, u32[]{:S(2)}) collective-permute-start(f32[512,640]{1,0:T(8,128)S(1)} %collective-permute-done.7.refs_3_), channel_id=1, source_target_pairs={{0,24},{8,0},{16,8},{24,16},{32,56},{40,32},{48,40},{56,48},{64,88... | collective-permute-start | bytes 3932168 | tf_op jit(solution)/shard_map/ppermute | solution.py:468
  360.6 74.2 %collective-permute-start.20 = (f32[1024,640]{1,0:T(8,128)S(1)}, f32[1024,640]{1,0:T(8,128)S(1)}, u32[]{:S(2)}, u32[]{:S(2)}) collective-permute-start(f32[1024,640]{1,0:T(8,128)S(1)} %get-tuple-element.113), channel_id=1, source_target_pairs={{0,8},{8,16},{16,24},{24,0},{32,40},{40,48},{48,56},{56,32},{64,72... | collective-permute-start | bytes 7864328 | tf_op jit(solution)/shard_map/ppermute | solution.py:468
  369.4 33.3 %collective-permute-start.24 = (f32[512,640]{1,0:T(8,128)}, f32[512,640]{1,0:T(8,128)S(1)}, u32[]{:S(2)}, u32[]{:S(2)}) collective-permute-start(f32[512,640]{1,0:T(8,128)} %collective-permute-done.12.refs_0_), channel_id=1, source_target_pairs={{0,24},{8,0},{16,8},{24,16},{32,56},{40,32},{48,40},{56,48},{64,88... | collective-permute-start | bytes 3932168 | tf_op jit(solution)/shard_map/ppermute | solution.py:468
  373.3 31.9 %collective-permute-start.25 = (f32[512,640]{1,0:T(8,128)}, f32[512,640]{1,0:T(8,128)S(1)}, u32[]{:S(2)}, u32[]{:S(2)}) collective-permute-start(f32[512,640]{1,0:T(8,128)} %collective-permute-done.13.refs_1_), channel_id=1, source_target_pairs={{0,96},{8,104},{16,112},{24,120},{32,0},{40,8},{48,16},{56,24},{64... | collective-permute-start | bytes 3932168 | tf_op jit(solution)/shard_map/ppermute | solution.py:468
  373.3 57.6 %collective-permute-start.26 = (f32[512,640]{1,0:T(8,128)}, f32[512,640]{1,0:T(8,128)S(1)}, u32[]{:S(2)}, u32[]{:S(2)}) collective-permute-start(f32[512,640]{1,0:T(8,128)} %collective-permute-done.14.refs_2_), channel_id=1, source_target_pairs={{0,24},{8,0},{16,8},{24,16},{32,56},{40,32},{48,40},{56,48},{64,88... | collective-permute-start | bytes 3932168 | tf_op jit(solution)/shard_map/ppermute | solution.py:468
  375.4 56.5 %collective-permute-start.27 = (f32[512,640]{1,0:T(8,128)}, f32[512,640]{1,0:T(8,128)S(1)}, u32[]{:S(2)}, u32[]{:S(2)}) collective-permute-start(f32[512,640]{1,0:T(8,128)} %collective-permute-done.15.refs_3_), channel_id=1, source_target_pairs={{0,96},{8,104},{16,112},{24,120},{32,0},{40,8},{48,16},{56,24},{64... | collective-permute-start | bytes 3932168 | tf_op jit(solution)/shard_map/ppermute | solution.py:468
  403.9 60.9 %collective-permute-start.21 = (f32[1024,640]{1,0:T(8,128)S(1)}, f32[1024,640]{1,0:T(8,128)S(1)}, u32[]{:S(2)}, u32[]{:S(2)}) collective-permute-start(f32[1024,640]{1,0:T(8,128)S(1)} %get-tuple-element.114), channel_id=1, source_target_pairs={{0,32},{8,40},{16,48},{24,56},{32,64},{40,72},{48,80},{56,88},{64,... | collective-permute-start | bytes 7864328 | tf_op jit(solution)/shard_map/ppermute | solution.py:468
  406.2 68.5 %collective-permute-start.22 = (f32[1024,640]{1,0:T(8,128)S(1)}, f32[1024,640]{1,0:T(8,128)S(1)}, u32[]{:S(2)}, u32[]{:S(2)}) collective-permute-start(f32[1024,640]{1,0:T(8,128)S(1)} %get-tuple-element.113), channel_id=1, source_target_pairs={{0,24},{8,0},{16,8},{24,16},{32,56},{40,32},{48,40},{56,48},{64,88... | collective-permute-start | bytes 7864328 | tf_op jit(solution)/shard_map/ppermute | solution.py:468
  431.9 44.9 %collective-permute-start.23 = (f32[1024,640]{1,0:T(8,128)S(1)}, f32[1024,640]{1,0:T(8,128)S(1)}, u32[]{:S(2)}, u32[]{:S(2)}) collective-permute-start(f32[1024,640]{1,0:T(8,128)S(1)} %get-tuple-element.114), channel_id=1, source_target_pairs={{0,96},{8,104},{16,112},{24,120},{32,0},{40,8},{48,16},{56,24},{64... | collective-permute-start | bytes 7864328 | tf_op jit(solution)/shard_map/ppermute | solution.py:468
  433.0 61.3 %collective-permute-start.28 = (f32[1024,640]{1,0:T(8,128)S(1)}, f32[1024,640]{1,0:T(8,128)S(1)}, u32[]{:S(2)}, u32[]{:S(2)}) collective-permute-start(f32[1024,640]{1,0:T(8,128)S(1)} %collective-permute-done.8.refs_0_), channel_id=1, source_target_pairs={{0,8},{8,16},{16,24},{24,0},{32,40},{40,48},{48,56},{56,32},{64,72... | collective-permute-start | bytes 7864328 | tf_op jit(solution)/shard_map/ppermute | solution.py:468
  434.8 86.2 %collective-permute-start.29 = (f32[1024,640]{1,0:T(8,128)}, f32[1024,640]{1,0:T(8,128)}, u32[]{:S(2)}, u32[]{:S(2)}) collective-permute-start(f32[1024,640]{1,0:T(8,128)} %collective-permute-done.9.refs_1_), channel_id=1, source_target_pairs={{0,32},{8,40},{16,48},{24,56},{32,64},{40,72},{48,80},{56,88},{64,... | collective-permute-start | bytes 7864328 | tf_op jit(solution)/shard_map/ppermute | solution.py:468
  464.7 65.2 %collective-permute-start.30 = (f32[512,640]{1,0:T(8,128)}, f32[512,640]{1,0:T(8,128)}, u32[]{:S(2)}, u32[]{:S(2)}) collective-permute-start(f32[512,640]{1,0:T(8,128)} %collective-permute-done.12.refs_0_), channel_id=1, source_target_pairs={{0,8},{8,16},{16,24},{24,0},{32,40},{40,48},{48,56},{56,32},{64,72... | collective-permute-start | bytes 3932168 | tf_op jit(solution)/shard_map/ppermute | solution.py:468
  476.1 73.0 %collective-permute-start.31 = (f32[512,640]{1,0:T(8,128)}, f32[512,640]{1,0:T(8,128)}, u32[]{:S(2)}, u32[]{:S(2)}) collective-permute-start(f32[512,640]{1,0:T(8,128)} %collective-permute-done.13.refs_1_), channel_id=1, source_target_pairs={{0,32},{8,40},{16,48},{24,56},{32,64},{40,72},{48,80},{56,88},{64,... | collective-permute-start | bytes 3932168 | tf_op jit(solution)/shard_map/ppermute | solution.py:468
  478.4 77.3 %collective-permute-start.32 = (f32[512,640]{1,0:T(8,128)}, f32[512,640]{1,0:T(8,128)}, u32[]{:S(2)}, u32[]{:S(2)}) collective-permute-start(f32[512,640]{1,0:T(8,128)} %collective-permute-done.14.refs_2_), channel_id=1, source_target_pairs={{0,8},{8,16},{16,24},{24,0},{32,40},{40,48},{48,56},{56,32},{64,72... | collective-permute-start | bytes 3932168 | tf_op jit(solution)/shard_map/ppermute | solution.py:468
  495.9 68.3 %collective-permute-start.33 = (f32[512,640]{1,0:T(8,128)}, f32[512,640]{1,0:T(8,128)}, u32[]{:S(2)}, u32[]{:S(2)}) collective-permute-start(f32[512,640]{1,0:T(8,128)} %collective-permute-done.15.refs_3_), channel_id=1, source_target_pairs={{0,32},{8,40},{16,48},{24,56},{32,64},{40,72},{48,80},{56,88},{64,... | collective-permute-start | bytes 3932168 | tf_op jit(solution)/shard_map/ppermute | solution.py:468
  550.4 17.6 %collective-permute-start.40 = (f32[448,640]{1,0:T(8,128)S(1)}, f32[448,640]{1,0:T(8,128)S(1)}, u32[]{:S(2)}, u32[]{:S(2)}) collective-permute-start(f32[448,640]{1,0:T(8,128)S(1)} %slice.80), channel_id=1, source_target_pairs={{0,8},{8,16},{16,24},{24,0},{32,40},{40,48},{48,56},{56,32},{64,72... | collective-permute-start | bytes 3440648 | tf_op jit(solution)/shard_map/ppermute | solution.py:468
  553.7 29.4 %collective-permute-start.41 = (f32[448,640]{1,0:T(8,128)S(1)}, f32[448,640]{1,0:T(8,128)S(1)}, u32[]{:S(2)}, u32[]{:S(2)}) collective-permute-start(f32[448,640]{1,0:T(8,128)S(1)} %slice.81), channel_id=1, source_target_pairs={{0,32},{8,40},{16,48},{24,56},{32,64},{40,72},{48,80},{56,88},{64,... | collective-permute-start | bytes 3440648 | tf_op jit(solution)/shard_map/ppermute | solution.py:468
  553.8 75.9 %collective-permute-start.34 = (f32[1024,640]{1,0:T(8,128)S(1)}, f32[1024,640]{1,0:T(8,128)S(1)}, u32[]{:S(2)}, u32[]{:S(2)}) collective-permute-start(f32[1024,640]{1,0:T(8,128)S(1)} %collective-permute-done.18.refs_0_), channel_id=1, source_target_pairs={{0,24},{8,0},{16,8},{24,16},{32,56},{40,32},{48,40},{56,48},{64,88... | collective-permute-start | bytes 7864328 | tf_op jit(solution)/shard_map/ppermute | solution.py:468
  555.7 75.7 %collective-permute-start.35 = (f32[1024,640]{1,0:T(8,128)S(1)}, f32[1024,640]{1,0:T(8,128)S(1)}, u32[]{:S(2)}, u32[]{:S(2)}) collective-permute-start(f32[1024,640]{1,0:T(8,128)S(1)} %collective-permute-done.19.refs_1_), channel_id=1, source_target_pairs={{0,96},{8,104},{16,112},{24,120},{32,0},{40,8},{48,16},{56,24},{64... | collective-permute-start | bytes 7864328 | tf_op jit(solution)/shard_map/ppermute | solution.py:468
  564.2 54.6 %collective-permute-start.38 = (f32[504,640]{1,0:T(8,128)S(1)}, f32[504,640]{1,0:T(8,128)S(1)}, u32[]{:S(2)}, u32[]{:S(2)}) collective-permute-start(f32[504,640]{1,0:T(8,128)S(1)} %slice.78), channel_id=1, source_target_pairs={{0,24},{8,0},{16,8},{24,16},{32,56},{40,32},{48,40},{56,48},{64,88... | collective-permute-start | bytes 3870728 | tf_op jit(solution)/shard_map/ppermute | solution.py:468
  568.1 48.0 %collective-permute-start.42 = (f32[448,640]{1,0:T(8,128)S(1)}, f32[448,640]{1,0:T(8,128)S(1)}, u32[]{:S(2)}, u32[]{:S(2)}) collective-permute-start(f32[448,640]{1,0:T(8,128)S(1)} %slice.82), channel_id=1, source_target_pairs={{0,24},{8,0},{16,8},{24,16},{32,56},{40,32},{48,40},{56,48},{64,88... | collective-permute-start | bytes 3440648 | tf_op jit(solution)/shard_map/ppermute | solution.py:468
  583.1 40.5 %collective-permute-start.39 = (f32[504,640]{1,0:T(8,128)S(1)}, f32[504,640]{1,0:T(8,128)S(1)}, u32[]{:S(2)}, u32[]{:S(2)}) collective-permute-start(f32[504,640]{1,0:T(8,128)S(1)} %slice.79), channel_id=1, source_target_pairs={{0,96},{8,104},{16,112},{24,120},{32,0},{40,8},{48,16},{56,24},{64... | collective-permute-start | bytes 3870728 | tf_op jit(solution)/shard_map/ppermute | solution.py:468
  617.1 19.0 %collective-permute-start.36 = (f32[520,640]{1,0:T(8,128)S(1)}, f32[520,640]{1,0:T(8,128)S(1)}, u32[]{:S(2)}, u32[]{:S(2)}) collective-permute-start(f32[520,640]{1,0:T(8,128)S(1)} %slice.76), channel_id=1, source_target_pairs={{0,8},{8,16},{16,24},{24,0},{32,40},{40,48},{48,56},{56,32},{64,72... | collective-permute-start | bytes 3993608 | tf_op jit(solution)/shard_map/ppermute | solution.py:468
  618.8 20.1 %collective-permute-start.37 = (f32[520,640]{1,0:T(8,128)S(1)}, f32[520,640]{1,0:T(8,128)S(1)}, u32[]{:S(2)}, u32[]{:S(2)}) collective-permute-start(f32[520,640]{1,0:T(8,128)S(1)} %slice.77), channel_id=1, source_target_pairs={{0,32},{8,40},{16,48},{24,56},{32,64},{40,72},{48,80},{56,88},{64,... | collective-permute-start | bytes 3993608 | tf_op jit(solution)/shard_map/ppermute | solution.py:468
  623.6 36.9 %collective-permute-start.43 = (f32[448,640]{1,0:T(8,128)}, f32[448,640]{1,0:T(8,128)}, u32[]{:S(2)}, u32[]{:S(2)}) collective-permute-start(f32[448,640]{1,0:T(8,128)} %slice.83), channel_id=1, source_target_pairs={{0,96},{8,104},{16,112},{24,120},{32,0},{40,8},{48,16},{56,24},{64... | collective-permute-start | bytes 3440648 | tf_op jit(solution)/shard_map/ppermute | solution.py:468
  629.7 35.5 %collective-permute-start.44 = (f32[64,640]{1,0:T(8,128)}, f32[64,640]{1,0:T(8,128)}, u32[]{:S(2)}, u32[]{:S(2)}) collective-permute-start(f32[64,640]{1,0:T(8,128)} %slice.84), channel_id=1, source_target_pairs={{0,8},{8,16},{16,24},{24,0},{32,40},{40,48},{48,56},{56,32},{64,72... | collective-permute-start | bytes 491528 | tf_op jit(solution)/shard_map/ppermute | solution.py:468
  632.9 32.3 %collective-permute-start.45 = (f32[64,640]{1,0:T(8,128)}, f32[64,640]{1,0:T(8,128)}, u32[]{:S(2)}, u32[]{:S(2)}) collective-permute-start(f32[64,640]{1,0:T(8,128)} %slice.85), channel_id=1, source_target_pairs={{0,32},{8,40},{16,48},{24,56},{32,64},{40,72},{48,80},{56,88},{64,... | collective-permute-start | bytes 491528 | tf_op jit(solution)/shard_map/ppermute | solution.py:468
  637.2 27.9 %collective-permute-start.46 = (f32[64,640]{1,0:T(8,128)}, f32[64,640]{1,0:T(8,128)}, u32[]{:S(2)}, u32[]{:S(2)}) collective-permute-start(f32[64,640]{1,0:T(8,128)} %slice.86), channel_id=1, source_target_pairs={{0,24},{8,0},{16,8},{24,16},{32,56},{40,32},{48,40},{56,48},{64,88... | collective-permute-start | bytes 491528 | tf_op jit(solution)/shard_map/ppermute | solution.py:468
  640.0 25.2 %collective-permute-start.47 = (f32[64,640]{1,0:T(8,128)}, f32[64,640]{1,0:T(8,128)}, u32[]{:S(2)}, u32[]{:S(2)}) collective-permute-start(f32[64,640]{1,0:T(8,128)} %slice.87), channel_id=1, source_target_pairs={{0,96},{8,104},{16,112},{24,120},{32,0},{40,8},{48,16},{56,24},{64... | collective-permute-start | bytes 491528 | tf_op jit(solution)/shard_map/ppermute | solution.py:468
  (30 other events, 140.1 us)
where the time goes:
time: 669 us; the launch traced here: 668 us
  waiting for transfers between devices  378 us (57%)
  Pallas kernels  184 us (28%)
  starting transfers between devices  71.5 us (11%)
  local copies, waits for them, and re-layouts  28.8 us (4%)
    ppermute x48, waiting for transfers between devices, send(): lax.ppermute(pair[k], 'dp', [(d, shift(d, dz, dy)) for d in range(N_DP)])  378 us
    pallas_call x1, Pallas kernels, front(): pl.pallas_call(kern, out_shape=tuple((jax.ShapeDtypeStruct(shape, kind) f...  105 us
    ppermute x48, starting transfers between devices, send(): lax.ppermute(pair[k], 'dp', [(d, shift(d, dz, dy)) for d in range(N_DP)])  71.5 us
    pallas_call x18, Pallas kernels, place(): pl.pallas_call(kern, out_shape=jax.ShapeDtypeStruct((vocab, dim), F32), i...  71.4 us
    unnamed x62, local copies, waits for them, and re-layouts  17.3 us
  transfers between devices with their start and end apart: 48, of which 22 were waited for; matrix products, arithmetic and copies ran while one was open for 2% of the time, Pallas kernels for 11%

commit v1 on v0

--- a/solution.py
+++ b/solution.py
@@ -11,8 +11,7 @@
 NORM_EPS = 1e-6
 SIDE, N_DP, N_TP, LANES = 4, 16, 8, 128
 UP, DOWN, AWAY = 1, 3, 2
-TILT = 8
-LAST = 64
+LAST = 128
 MIB = 2 ** 20
 L_FRONT = 41
 MESH = pl.DeviceIdType.MESH
@@ -113,6 +112,7 @@
         for i in range(per):
             tab_copy(i).start()
         own_tab.start()
+        all_ref[...] = jnp.zeros(all_ref.shape, F32)
         barrier = pltpu.get_barrier_semaphore()
         for dz, dy in ORDER[:-1]:
             pl.semaphore_signal(barrier, inc=1, device_id=(at[dz, dy], col), device_id_type=MESH)
@@ -273,7 +273,7 @@
         line = jnp.transpose(square[...])[0:few]
         own_row[...] = line
         all_ref[me] = line
-        dp_sent, dp_came = to_dp(own_row, all_ref, 2)
+        dp_sent, dp_came = to_dp(own_row, all_ref, 2, pl.ds(0, SIDE))
         twin = col + 1 - 2 * lax.rem(col, 2)
         pay_came()
         mask_came()
@@ -521,8 +521,7 @@
     settle(put(low_side[DOWN], DOWN, UP))
 
     high_side[UP], high_side[DOWN] = wait(high_side[UP], high_side[DOWN])
-    cut = quarter + TILT
-    high_far = [send([x[:cut] for x in high_side[UP]], 1, UP), send([x[cut:] for x in high_side[DOWN]], 1, DOWN)]
+    high_far = [send([x[:quarter] for x in high_side[UP]], 1, UP), send([x[quarter:] for x in high_side[DOWN]], 1, DOWN)]
     settle(put(high_side[UP], UP, DOWN))
     settle(put(high_side[DOWN], UP, UP))
 
@@ -541,7 +540,7 @@
     settle(put(low_far, DOWN, AWAY))
 
     high_far = wait(*high_far)
-    settle(put(high_far[0], UP, AWAY, 0), put(high_far[1], UP, AWAY, cut))
+    settle(put(high_far[0], UP, AWAY, 0), put(high_far[1], UP, AWAY, quarter))
     for up, down, end in zip(last_up, last_down, ends):
         up, down = wait(up, down)
         settle(put(up, AWAY, AWAY, end.start), put(down, AWAY, AWAY, quarter + end.start))

time: 669 us -> 640 us (0.957)
  starting transfers between devices: 71.5 us -> 56.8 us
  local copies, waits for them, and re-layouts: 28.8 us -> 19.3 us
    ppermute x48, starting transfers between devices: 71.5 us -> 56.8 us  [send(): lax.ppermute(pair[k], 'dp', [(d, shift(d, dz, dy)) for d in range(N_DP)])]
    unnamed x62 -> x46, local copies, waits for them, and re-layouts: 17.3 us -> 9.89 us
  transfers between devices with their start and end apart: 48 -> 48, of which waited for: 22 -> 18; matrix products, arithmetic and copies ran while one was open for 2% -> 2% of each run, Pallas kernels for 11% -> 12%
where the time goes in v1:
time: 640 us; the launch traced here: 639 us
  waiting for transfers between devices  373 us (58%)
  Pallas kernels  183 us (29%)
  starting transfers between devices  56.8 us (9%)
  local copies, waits for them, and re-layouts  19.3 us (3%)
    ppermute x48, waiting for transfers between devices, send(): lax.ppermute(pair[k], 'dp', [(d, shift(d, dz, dy)) for d in range(N_DP)])  373 us
    pallas_call x1, Pallas kernels, front(): pl.pallas_call(kern, out_shape=tuple((jax.ShapeDtypeStruct(shape, kind) f...  105 us
    pallas_call x18, Pallas kernels, place(): pl.pallas_call(kern, out_shape=jax.ShapeDtypeStruct((vocab, dim), F32), i...  70.6 us
    ppermute x48, starting transfers between devices, send(): lax.ppermute(pair[k], 'dp', [(d, shift(d, dz, dy)) for d in range(N_DP)])  56.8 us
  transfers between devices with their start and end apart: 48, of which 18 were waited for; matrix products, arithmetic and copies ran while one was open for 2% of the time, Pallas kernels for 12%

profile of v1, /device:TPU:0, one launch (start us, length us, event | category | flops | bytes accessed | tf_op | source)
XLA Modules:
  0.0 638.8 jit_solution(7603422488334197576)
XLA Ops:
  0.6 105.4 %front.1 = (f32[16,64,1024]{2,1,0:T(8,128)S(1)}, f32[2,512,640]{2,1,0:T(8,128)S(1)}, bf16[1024,640]{1,0:T(8,128)(2,1)S(1)}, bf16[2048,640]{1,0:T(8,128)(2,1)S(1)...) custom-call(bf16[64,640]{1,0:T(8,128)(2,1)} %hid_hbm.1, ...), custom_call_target="tpu_custom_call" | custom-call | flops 3000000000 | bytes 104857600 | tf_op jit(solution)/shard_map/front/pallas_call | solution.py:379
  108.0 3.2 collective-permute-start.2
  112.8 7.2 %finish.1 = f32[2,512,640]{2,1,0:T(8,128)S(1)} custom-call(f32[16,64,1024]{2,1,0:T(8,128)S(1)} %get-tuple-element.84.tea_ref, bf16[1024,640]{1,0:T(8,128)(2,1)S(1)} %get-tuple-element.85.x_ref, bf16[2048,640]{1,0:T(8,128)(2,1)S(1)} %get-tuple-element.86.tab_ref, f32[128,128]{1,0:T(8,128)S(1)} %get-tuple-element.87.coef_ref), custom_call_target="tpu_custom_call" | custom-call | flops 1000000000 | bytes 8388608 | tf_op jit(solution)/shard_map/finish/pallas_call | solution.py:412
  120.5 18.7 %collective-permute-done.refs_0_ = f32[512,640]{1,0:T(8,128)S(1)} collective-permute-done((f32[512,640]{1,0:T(8,128)S(1)}, f32[512,640]{1,0:T(8,128)S(1)}, u32[]{:S(2)}, u32[]{:S(2)}) %collective-permute-start) | collective-permute-done | bytes 1310752 | tf_op jit(solution)/shard_map/ppermute | solution.py:468
  144.6 22.7 %collective-permute-done.4.refs_0_ = f32[512,640]{1,0:T(8,128)S(1)} collective-permute-done((f32[512,640]{1,0:T(8,128)S(1)}, f32[512,640]{1,0:T(8,128)S(1)}, u32[]{:S(2)}, u32[]{:S(2)}) %collective-permute-start.4) | collective-permute-done | bytes 1310752 | tf_op jit(solution)/shard_map/ppermute | solution.py:468
  168.8 3.2 collective-permute-done.5.refs_1_
  174.3 4.1 place.18.refs_4_
  178.4 70.7 %collective-permute-done.7.refs_3_ = f32[512,640]{1,0:T(8,128)S(1)} collective-permute-done((f32[512,640]{1,0:T(8,128)S(1)}, f32[512,640]{1,0:T(8,128)S(1)}, u32[]{:S(2)}, u32[]{:S(2)}) %collective-permute-start.7) | collective-permute-done | bytes 1310752 | tf_op jit(solution)/shard_map/ppermute | solution.py:468
  249.1 4.1 place.19.refs_4_
  254.9 3.2 collective-permute-start.14
  264.1 17.9 %collective-permute-done.12.refs_0_ = f32[512,640]{1,0:T(8,128)S(1)} collective-permute-done((f32[512,640]{1,0:T(8,128)S(1)}, f32[512,640]{1,0:T(8,128)S(1)}, u32[]{:S(2)}, u32[]{:S(2)}) %collective-permute-start.12) | collective-permute-done | bytes 1310752 | tf_op jit(solution)/shard_map/ppermute | solution.py:468
  282.0 3.7 collective-permute-start.18
  288.8 3.2 collective-permute-start.19
  292.0 4.1 place.20.refs_2_
  296.5 4.1 place.21.refs_2_
  300.6 4.1 place.22.refs_4_
  304.8 62.4 %collective-permute-done.15.refs_3_ = f32[512,640]{1,0:T(8,128)} collective-permute-done((f32[512,640]{1,0:T(8,128)S(1)}, f32[512,640]{1,0:T(8,128)}, u32[]{:S(2)}, u32[]{:S(2)}) %collective-permute-start.15) | collective-permute-done | bytes 1310752 | tf_op jit(solution)/shard_map/ppermute | solution.py:468
  367.2 3.8 collective-permute-start.24
  371.1 3.2 collective-permute-start.26
  374.4 25.8 %collective-permute-done.24.refs_0_ = f32[512,640]{1,0:T(8,128)S(1)} collective-permute-done((f32[512,640]{1,0:T(8,128)S(1)}, f32[512,640]{1,0:T(8,128)S(1)}, u32[]{:S(2)}, u32[]{:S(2)}) %collective-permute-start.24) | collective-permute-done | bytes 1310752 | tf_op jit(solution)/shard_map/ppermute | solution.py:468
  400.2 24.3 %collective-permute-done.26.refs_2_ = f32[512,640]{1,0:T(8,128)S(1)} collective-permute-done((f32[512,640]{1,0:T(8,128)}, f32[512,640]{1,0:T(8,128)S(1)}, u32[]{:S(2)}, u32[]{:S(2)}) %collective-permute-start.26) | collective-permute-done | bytes 1310752 | tf_op jit(solution)/shard_map/ppermute | solution.py:468
  424.4 3.6 collective-permute-start.22
  429.1 27.0 %collective-permute-done.30.refs_0_ = f32[512,640]{1,0:T(8,128)S(1)} collective-permute-done((f32[512,640]{1,0:T(8,128)S(1)}, f32[512,640]{1,0:T(8,128)S(1)}, u32[]{:S(2)}, u32[]{:S(2)}) %collective-permute-start.30) | collective-permute-done | bytes 1310752 | tf_op jit(solution)/shard_map/ppermute | solution.py:468
  457.3 4.2 place.23.refs_2_
  461.5 2.3 collective-permute-start.34
  463.8 21.5 %collective-permute-done.22.refs_0_ = f32[1024,640]{1,0:T(8,128)S(1)} collective-permute-done((f32[1024,640]{1,0:T(8,128)S(1)}, f32[1024,640]{1,0:T(8,128)S(1)}, u32[]{:S(2)}, u32[]{:S(2)}) %collective-permute-start.22) | collective-permute-done | bytes 2621472 | tf_op jit(solution)/shard_map/ppermute | solution.py:468
  485.3 26.3 %collective-permute-done.28.refs_0_ = f32[1024,640]{1,0:T(8,128)S(1)} collective-permute-done((f32[1024,640]{1,0:T(8,128)S(1)}, f32[1024,640]{1,0:T(8,128)S(1)}, u32[]{:S(2)}, u32[]{:S(2)}) %collective-permute-start.28) | collective-permute-done | bytes 2621472 | tf_op jit(solution)/shard_map/ppermute | solution.py:468
  511.6 6.6 %collective-permute-done.29.refs_1_ = f32[1024,640]{1,0:T(8,128)S(1)} collective-permute-done((f32[1024,640]{1,0:T(8,128)S(1)}, f32[1024,640]{1,0:T(8,128)S(1)}, u32[]{:S(2)}, u32[]{:S(2)}) %collective-permute-start.29) | collective-permute-done | bytes 2621472 | tf_op jit(solution)/shard_map/ppermute | solution.py:468
  518.2 4.1 place.24.refs_2_
  522.4 4.6 place.25.refs_2_
  527.0 4.1 place.26.refs_2_
  531.2 4.1 place.27.refs_4_
  536.7 4.1 place.28.refs_2_
  540.8 4.1 place.29.refs_2_
  548.5 21.6 %collective-permute-done.33.refs_1_ = f32[512,640]{1,0:T(8,128)} collective-permute-done((f32[512,640]{1,0:T(8,128)}, f32[512,640]{1,0:T(8,128)}, u32[]{:S(2)}, u32[]{:S(2)}) %collective-permute-start.33) | collective-permute-done | bytes 1310752 | tf_op jit(solution)/shard_map/ppermute | solution.py:468
  570.1 2.5 collective-permute-start.42
  573.1 11.0 %collective-permute-done.41.refs_1_ = f32[384,640]{1,0:T(8,128)S(1)} collective-permute-done((f32[384,640]{1,0:T(8,128)S(1)}, f32[384,640]{1,0:T(8,128)S(1)}, u32[]{:S(2)}, u32[]{:S(2)}) %collective-permute-start.41) | collective-permute-done | bytes 983072 | tf_op jit(solution)/shard_map/ppermute | solution.py:468
  584.1 3.7 collective-permute-done.42.refs_2_
  587.8 3.7 collective-permute-start.38
  596.7 6.2 collective-permute-done.37.refs_1_
  604.0 2.6 collective-permute-done.38.refs_2_
  607.7 3.7 collective-permute-start.46
  616.4 3.1 place.30.refs_2_
  619.5 2.6 place.31.refs_2_
  622.2 4.8 place.32.refs_4_
  627.7 4.1 place.33.refs_4_
  631.9 3.7 place.34.refs_4_
  635.6 2.1 place.35
  (136 shorter events, 43.8 us)
Async XLA Ops:
  106.2 32.9 %collective-permute-start = (f32[512,640]{1,0:T(8,128)S(1)}, f32[512,640]{1,0:T(8,128)S(1)}, u32[]{:S(2)}, u32[]{:S(2)}) collective-permute-start(f32[512,640]{1,0:T(8,128)S(1)} %get-tuple-element.82.refs_0_), channel_id=1, source_target_pairs={{0,32},{8,40},{16,48},{24,56},{32,64},{40,72},{48,80},{56,88},{64,... | collective-permute-start | bytes 3932168 | tf_op jit(solution)/shard_map/ppermute | solution.py:468
  107.5 33.4 %collective-permute-start.1 = (f32[512,640]{1,0:T(8,128)S(1)}, f32[512,640]{1,0:T(8,128)S(1)}, u32[]{:S(2)}, u32[]{:S(2)}) collective-permute-start(f32[512,640]{1,0:T(8,128)S(1)} %get-tuple-element.83.refs_1_), channel_id=1, source_target_pairs={{0,8},{8,16},{16,24},{24,0},{32,40},{40,48},{48,56},{56,32},{64,72... | collective-permute-start | bytes 3932168 | tf_op jit(solution)/shard_map/ppermute | solution.py:468
  108.0 33.6 %collective-permute-start.2 = (f32[512,640]{1,0:T(8,128)S(1)}, f32[512,640]{1,0:T(8,128)S(1)}, u32[]{:S(2)}, u32[]{:S(2)}) collective-permute-start(f32[512,640]{1,0:T(8,128)S(1)} %get-tuple-element.82.refs_0_), channel_id=1, source_target_pairs={{0,96},{8,104},{16,112},{24,120},{32,0},{40,8},{48,16},{56,24},{64... | collective-permute-start | bytes 3932168 | tf_op jit(solution)/shard_map/ppermute | solution.py:468
  111.1 32.2 %collective-permute-start.3 = (f32[512,640]{1,0:T(8,128)S(1)}, f32[512,640]{1,0:T(8,128)S(1)}, u32[]{:S(2)}, u32[]{:S(2)}) collective-permute-start(f32[512,640]{1,0:T(8,128)S(1)} %get-tuple-element.83.refs_1_), channel_id=1, source_target_pairs={{0,24},{8,0},{16,8},{24,16},{32,56},{40,32},{48,40},{56,48},{64,88... | collective-permute-start | bytes 3932168 | tf_op jit(solution)/shard_map/ppermute | solution.py:468
  120.2 47.1 %collective-permute-start.4 = (f32[512,640]{1,0:T(8,128)S(1)}, f32[512,640]{1,0:T(8,128)S(1)}, u32[]{:S(2)}, u32[]{:S(2)}) collective-permute-start(f32[512,640]{1,0:T(8,128)S(1)} %get-tuple-element.153.refs_2_), channel_id=1, source_target_pairs={{0,32},{8,40},{16,48},{24,56},{32,64},{40,72},{48,80},{56,88},{64,... | collective-permute-start | bytes 3932168 | tf_op jit(solution)/shard_map/ppermute | solution.py:468
  139.2 32.9 %collective-permute-start.5 = (f32[512,640]{1,0:T(8,128)S(1)}, f32[512,640]{1,0:T(8,128)S(1)}, u32[]{:S(2)}, u32[]{:S(2)}) collective-permute-start(f32[512,640]{1,0:T(8,128)S(1)} %get-tuple-element.152.refs_3_), channel_id=1, source_target_pairs={{0,8},{8,16},{16,24},{24,0},{32,40},{40,48},{48,56},{56,32},{64,72... | collective-permute-start | bytes 3932168 | tf_op jit(solution)/shard_map/ppermute | solution.py:468
  140.9 31.5 %collective-permute-start.6 = (f32[512,640]{1,0:T(8,128)S(1)}, f32[512,640]{1,0:T(8,128)S(1)}, u32[]{:S(2)}, u32[]{:S(2)}) collective-permute-start(f32[512,640]{1,0:T(8,128)S(1)} %get-tuple-element.153.refs_2_), channel_id=1, source_target_pairs={{0,96},{8,104},{16,112},{24,120},{32,0},{40,8},{48,16},{56,24},{64... | collective-permute-start | bytes 3932168 | tf_op jit(solution)/shard_map/ppermute | solution.py:468
  141.6 111.6 %collective-permute-start.8 = (f32[1024,640]{1,0:T(8,128)S(1)}, f32[1024,640]{1,0:T(8,128)S(1)}, u32[]{:S(2)}, u32[]{:S(2)}) collective-permute-start(f32[1024,640]{1,0:T(8,128)S(1)} %pad_maximum_fusion), channel_id=1, source_target_pairs={{0,8},{8,16},{16,24},{24,0},{32,40},{40,48},{48,56},{56,32},{64,72... | collective-permute-start | bytes 7864328 | tf_op jit(solution)/shard_map/ppermute | solution.py:468
  143.3 111.6 %collective-permute-start.9 = (f32[1024,640]{1,0:T(8,128)S(1)}, f32[1024,640]{1,0:T(8,128)S(1)}, u32[]{:S(2)}, u32[]{:S(2)}) collective-permute-start(f32[1024,640]{1,0:T(8,128)S(1)} %pad_maximum_fusion.1), channel_id=1, source_target_pairs={{0,32},{8,40},{16,48},{24,56},{32,64},{40,72},{48,80},{56,88},{64,... | collective-permute-start | bytes 7864328 | tf_op jit(solution)/shard_map/ppermute | solution.py:468
  167.3 93.2 %collective-permute-start.10 = (f32[1024,640]{1,0:T(8,128)S(1)}, f32[1024,640]{1,0:T(8,128)S(1)}, u32[]{:S(2)}, u32[]{:S(2)}) collective-permute-start(f32[1024,640]{1,0:T(8,128)S(1)} %pad_maximum_fusion), channel_id=1, source_target_pairs={{0,24},{8,0},{16,8},{24,16},{32,56},{40,32},{48,40},{56,48},{64,88... | collective-permute-start | bytes 7864328 | tf_op jit(solution)/shard_map/ppermute | solution.py:468
  172.0 92.1 %collective-permute-start.11 = (f32[1024,640]{1,0:T(8,128)S(1)}, f32[1024,640]{1,0:T(8,128)S(1)}, u32[]{:S(2)}, u32[]{:S(2)}) collective-permute-start(f32[1024,640]{1,0:T(8,128)S(1)} %pad_maximum_fusion.1), channel_id=1, source_target_pairs={{0,96},{8,104},{16,112},{24,120},{32,0},{40,8},{48,16},{56,24},{64... | collective-permute-start | bytes 7864328 | tf_op jit(solution)/shard_map/ppermute | solution.py:468
  172.4 76.7 %collective-permute-start.7 = (f32[512,640]{1,0:T(8,128)S(1)}, f32[512,640]{1,0:T(8,128)S(1)}, u32[]{:S(2)}, u32[]{:S(2)}) collective-permute-start(f32[512,640]{1,0:T(8,128)S(1)} %get-tuple-element.152.refs_3_), channel_id=1, source_target_pairs={{0,24},{8,0},{16,8},{24,16},{32,56},{40,32},{48,40},{56,48},{64,88... | collective-permute-start | bytes 3932168 | tf_op jit(solution)/shard_map/ppermute | solution.py:468
  249.1 32.9 %collective-permute-start.12 = (f32[512,640]{1,0:T(8,128)S(1)}, f32[512,640]{1,0:T(8,128)S(1)}, u32[]{:S(2)}, u32[]{:S(2)}) collective-permute-start(f32[512,640]{1,0:T(8,128)S(1)} %collective-permute-done.refs_0_), channel_id=1, source_target_pairs={{0,32},{8,40},{16,48},{24,56},{32,64},{40,72},{48,80},{56,88},{64,... | collective-permute-start | bytes 3932168 | tf_op jit(solution)/shard_map/ppermute | solution.py:468
  253.2 33.5 %collective-permute-start.13 = (f32[512,640]{1,0:T(8,128)S(1)}, f32[512,640]{1,0:T(8,128)}, u32[]{:S(2)}, u32[]{:S(2)}) collective-permute-start(f32[512,640]{1,0:T(8,128)S(1)} %collective-permute-done.1.refs_1_), channel_id=1, source_target_pairs={{0,8},{8,16},{16,24},{24,0},{32,40},{40,48},{48,56},{56,32},{64,72... | collective-permute-start | bytes 3932168 | tf_op jit(solution)/shard_map/ppermute | solution.py:468
  254.9 33.8 %collective-permute-start.14 = (f32[512,640]{1,0:T(8,128)S(1)}, f32[512,640]{1,0:T(8,128)}, u32[]{:S(2)}, u32[]{:S(2)}) collective-permute-start(f32[512,640]{1,0:T(8,128)S(1)} %collective-permute-done.6.refs_2_), channel_id=1, source_target_pairs={{0,96},{8,104},{16,112},{24,120},{32,0},{40,8},{48,16},{56,24},{64... | collective-permute-start | bytes 3932168 | tf_op jit(solution)/shard_map/ppermute | solution.py:468
  260.5 110.5 %collective-permute-start.16 = (f32[1024,640]{1,0:T(8,128)}, f32[1024,640]{1,0:T(8,128)S(1)}, u32[]{:S(2)}, u32[]{:S(2)}) collective-permute-start(f32[1024,640]{1,0:T(8,128)} %constant_dynamic-update-slice_fusion), channel_id=1, source_target_pairs={{0,8},{8,16},{16,24},{24,0},{32,40},{40,48},{48,56},{56,32},{64,72... | collective-permute-start | bytes 7864328 | tf_op jit(solution)/shard_map/ppermute | solution.py:468
  264.1 106.9 %collective-permute-start.17 = (f32[1024,640]{1,0:T(8,128)}, f32[1024,640]{1,0:T(8,128)S(1)}, u32[]{:S(2)}, u32[]{:S(2)}) collective-permute-start(f32[1024,640]{1,0:T(8,128)} %constant_dynamic-update-slice_fusion.2), channel_id=1, source_target_pairs={{0,32},{8,40},{16,48},{24,56},{32,64},{40,72},{48,80},{56,88},{64,... | collective-permute-start | bytes 7864328 | tf_op jit(solution)/shard_map/ppermute | solution.py:468
  282.0 89.1 %collective-permute-start.18 = (f32[1024,640]{1,0:T(8,128)}, f32[1024,640]{1,0:T(8,128)}, u32[]{:S(2)}, u32[]{:S(2)}) collective-permute-start(f32[1024,640]{1,0:T(8,128)} %constant_dynamic-update-slice_fusion), channel_id=1, source_target_pairs={{0,24},{8,0},{16,8},{24,16},{32,56},{40,32},{48,40},{56,48},{64,88... | collective-permute-start | bytes 7864328 | tf_op jit(solution)/shard_map/ppermute | solution.py:468
  286.7 80.5 %collective-permute-start.15 = (f32[512,640]{1,0:T(8,128)S(1)}, f32[512,640]{1,0:T(8,128)}, u32[]{:S(2)}, u32[]{:S(2)}) collective-permute-start(f32[512,640]{1,0:T(8,128)S(1)} %collective-permute-done.7.refs_3_), channel_id=1, source_target_pairs={{0,24},{8,0},{16,8},{24,16},{32,56},{40,32},{48,40},{56,48},{64,88... | collective-permute-start | bytes 3932168 | tf_op jit(solution)/shard_map/ppermute | solution.py:468
  288.8 85.5 %collective-permute-start.19 = (f32[1024,640]{1,0:T(8,128)}, f32[1024,640]{1,0:T(8,128)}, u32[]{:S(2)}, u32[]{:S(2)}) collective-permute-start(f32[1024,640]{1,0:T(8,128)} %constant_dynamic-update-slice_fusion.2), channel_id=1, source_target_pairs={{0,96},{8,104},{16,112},{24,120},{32,0},{40,8},{48,16},{56,24},{64... | collective-permute-start | bytes 7864328 | tf_op jit(solution)/shard_map/ppermute | solution.py:468
  367.2 33.0 %collective-permute-start.24 = (f32[512,640]{1,0:T(8,128)S(1)}, f32[512,640]{1,0:T(8,128)S(1)}, u32[]{:S(2)}, u32[]{:S(2)}) collective-permute-start(f32[512,640]{1,0:T(8,128)S(1)} %collective-permute-done.12.refs_0_), channel_id=1, source_target_pairs={{0,24},{8,0},{16,8},{24,16},{32,56},{40,32},{48,40},{56,48},{64,88... | collective-permute-start | bytes 3932168 | tf_op jit(solution)/shard_map/ppermute | solution.py:468
  371.0 85.1 %collective-permute-start.20 = (f32[1024,640]{1,0:T(8,128)S(1)}, f32[1024,640]{1,0:T(8,128)S(1)}, u32[]{:S(2)}, u32[]{:S(2)}) collective-permute-start(f32[1024,640]{1,0:T(8,128)S(1)} %get-tuple-element.113), channel_id=1, source_target_pairs={{0,8},{8,16},{16,24},{24,0},{32,40},{40,48},{48,56},{56,32},{64,72... | collective-permute-start | bytes 7864328 | tf_op jit(solution)/shard_map/ppermute | solution.py:468
  371.0 29.2 %collective-permute-start.25 = (f32[512,640]{1,0:T(8,128)}, f32[512,640]{1,0:T(8,128)S(1)}, u32[]{:S(2)}, u32[]{:S(2)}) collective-permute-start(f32[512,640]{1,0:T(8,128)} %collective-permute-done.13.refs_1_), channel_id=1, source_target_pairs={{0,96},{8,104},{16,112},{24,120},{32,0},{40,8},{48,16},{56,24},{64... | collective-permute-start | bytes 3932168 | tf_op jit(solution)/shard_map/ppermute | solution.py:468
  371.1 53.3 %collective-permute-start.26 = (f32[512,640]{1,0:T(8,128)}, f32[512,640]{1,0:T(8,128)S(1)}, u32[]{:S(2)}, u32[]{:S(2)}) collective-permute-start(f32[512,640]{1,0:T(8,128)} %collective-permute-done.14.refs_2_), channel_id=1, source_target_pairs={{0,24},{8,0},{16,8},{24,16},{32,56},{40,32},{48,40},{56,48},{64,88... | collective-permute-start | bytes 3932168 | tf_op jit(solution)/shard_map/ppermute | solution.py:468
  374.3 53.7 %collective-permute-start.27 = (f32[512,640]{1,0:T(8,128)}, f32[512,640]{1,0:T(8,128)S(1)}, u32[]{:S(2)}, u32[]{:S(2)}) collective-permute-start(f32[512,640]{1,0:T(8,128)} %collective-permute-done.15.refs_3_), channel_id=1, source_target_pairs={{0,96},{8,104},{16,112},{24,120},{32,0},{40,8},{48,16},{56,24},{64... | collective-permute-start | bytes 3932168 | tf_op jit(solution)/shard_map/ppermute | solution.py:468
  400.2 56.0 %collective-permute-start.30 = (f32[512,640]{1,0:T(8,128)S(1)}, f32[512,640]{1,0:T(8,128)S(1)}, u32[]{:S(2)}, u32[]{:S(2)}) collective-permute-start(f32[512,640]{1,0:T(8,128)S(1)} %collective-permute-done.12.refs_0_), channel_id=1, source_target_pairs={{0,8},{8,16},{16,24},{24,0},{32,40},{40,48},{48,56},{56,32},{64,72... | collective-permute-start | bytes 3932168 | tf_op jit(solution)/shard_map/ppermute | solution.py:468
  400.2 61.3 %collective-permute-start.21 = (f32[1024,640]{1,0:T(8,128)S(1)}, f32[1024,640]{1,0:T(8,128)S(1)}, u32[]{:S(2)}, u32[]{:S(2)}) collective-permute-start(f32[1024,640]{1,0:T(8,128)S(1)} %get-tuple-element.114), channel_id=1, source_target_pairs={{0,32},{8,40},{16,48},{24,56},{32,64},{40,72},{48,80},{56,88},{64,... | collective-permute-start | bytes 7864328 | tf_op jit(solution)/shard_map/ppermute | solution.py:468
  424.4 60.8 %collective-permute-start.22 = (f32[1024,640]{1,0:T(8,128)S(1)}, f32[1024,640]{1,0:T(8,128)S(1)}, u32[]{:S(2)}, u32[]{:S(2)}) collective-permute-start(f32[1024,640]{1,0:T(8,128)S(1)} %get-tuple-element.113), channel_id=1, source_target_pairs={{0,24},{8,0},{16,8},{24,16},{32,56},{40,32},{48,40},{56,48},{64,88... | collective-permute-start | bytes 7864328 | tf_op jit(solution)/shard_map/ppermute | solution.py:468
  429.1 56.2 %collective-permute-start.23 = (f32[1024,640]{1,0:T(8,128)S(1)}, f32[1024,640]{1,0:T(8,128)S(1)}, u32[]{:S(2)}, u32[]{:S(2)}) collective-permute-start(f32[1024,640]{1,0:T(8,128)S(1)} %get-tuple-element.114), channel_id=1, source_target_pairs={{0,96},{8,104},{16,112},{24,120},{32,0},{40,8},{48,16},{56,24},{64... | collective-permute-start | bytes 7864328 | tf_op jit(solution)/shard_map/ppermute | solution.py:468
  456.1 55.5 %collective-permute-start.28 = (f32[1024,640]{1,0:T(8,128)S(1)}, f32[1024,640]{1,0:T(8,128)S(1)}, u32[]{:S(2)}, u32[]{:S(2)}) collective-permute-start(f32[1024,640]{1,0:T(8,128)S(1)} %collective-permute-done.8.refs_0_), channel_id=1, source_target_pairs={{0,8},{8,16},{16,24},{24,0},{32,40},{40,48},{48,56},{56,32},{64,72... | collective-permute-start | bytes 7864328 | tf_op jit(solution)/shard_map/ppermute | solution.py:468
  457.3 60.9 %collective-permute-start.29 = (f32[1024,640]{1,0:T(8,128)S(1)}, f32[1024,640]{1,0:T(8,128)S(1)}, u32[]{:S(2)}, u32[]{:S(2)}) collective-permute-start(f32[1024,640]{1,0:T(8,128)S(1)} %collective-permute-done.9.refs_1_), channel_id=1, source_target_pairs={{0,32},{8,40},{16,48},{24,56},{32,64},{40,72},{48,80},{56,88},{64,... | collective-permute-start | bytes 7864328 | tf_op jit(solution)/shard_map/ppermute | solution.py:468
  461.5 129.9 %collective-permute-start.34 = (f32[1024,640]{1,0:T(8,128)}, f32[1024,640]{1,0:T(8,128)}, u32[]{:S(2)}, u32[]{:S(2)}) collective-permute-start(f32[1024,640]{1,0:T(8,128)} %collective-permute-done.18.refs_0_), channel_id=1, source_target_pairs={{0,24},{8,0},{16,8},{24,16},{32,56},{40,32},{48,40},{56,48},{64,88... | collective-permute-start | bytes 7864328 | tf_op jit(solution)/shard_map/ppermute | solution.py:468
  485.3 59.7 %collective-permute-start.31 = (f32[512,640]{1,0:T(8,128)}, f32[512,640]{1,0:T(8,128)}, u32[]{:S(2)}, u32[]{:S(2)}) collective-permute-start(f32[512,640]{1,0:T(8,128)} %collective-permute-done.13.refs_1_), channel_id=1, source_target_pairs={{0,32},{8,40},{16,48},{24,56},{32,64},{40,72},{48,80},{56,88},{64,... | collective-permute-start | bytes 3932168 | tf_op jit(solution)/shard_map/ppermute | solution.py:468
  485.3 61.1 %collective-permute-start.32 = (f32[512,640]{1,0:T(8,128)}, f32[512,640]{1,0:T(8,128)}, u32[]{:S(2)}, u32[]{:S(2)}) collective-permute-start(f32[512,640]{1,0:T(8,128)} %collective-permute-done.14.refs_2_), channel_id=1, source_target_pairs={{0,8},{8,16},{16,24},{24,0},{32,40},{40,48},{48,56},{56,32},{64,72... | collective-permute-start | bytes 3932168 | tf_op jit(solution)/shard_map/ppermute | solution.py:468
  511.6 58.5 %collective-permute-start.33 = (f32[512,640]{1,0:T(8,128)}, f32[512,640]{1,0:T(8,128)}, u32[]{:S(2)}, u32[]{:S(2)}) collective-permute-start(f32[512,640]{1,0:T(8,128)} %collective-permute-done.15.refs_3_), channel_id=1, source_target_pairs={{0,32},{8,40},{16,48},{24,56},{32,64},{40,72},{48,80},{56,88},{64,... | collective-permute-start | bytes 3932168 | tf_op jit(solution)/shard_map/ppermute | solution.py:468
  518.2 74.3 %collective-permute-start.35 = (f32[1024,640]{1,0:T(8,128)}, f32[1024,640]{1,0:T(8,128)}, u32[]{:S(2)}, u32[]{:S(2)}) collective-permute-start(f32[1024,640]{1,0:T(8,128)} %collective-permute-done.19.refs_1_), channel_id=1, source_target_pairs={{0,96},{8,104},{16,112},{24,120},{32,0},{40,8},{48,16},{56,24},{64... | collective-permute-start | bytes 7864328 | tf_op jit(solution)/shard_map/ppermute | solution.py:468
  545.1 27.9 %collective-permute-start.40 = (f32[384,640]{1,0:T(8,128)S(1)}, f32[384,640]{1,0:T(8,128)S(1)}, u32[]{:S(2)}, u32[]{:S(2)}) collective-permute-start(f32[384,640]{1,0:T(8,128)S(1)} %slice.80), channel_id=1, source_target_pairs={{0,8},{8,16},{16,24},{24,0},{32,40},{40,48},{48,56},{56,32},{64,72... | collective-permute-start | bytes 2949128 | tf_op jit(solution)/shard_map/ppermute | solution.py:468
  546.4 37.6 %collective-permute-start.41 = (f32[384,640]{1,0:T(8,128)S(1)}, f32[384,640]{1,0:T(8,128)S(1)}, u32[]{:S(2)}, u32[]{:S(2)}) collective-permute-start(f32[384,640]{1,0:T(8,128)S(1)} %slice.81), channel_id=1, source_target_pairs={{0,32},{8,40},{16,48},{24,56},{32,64},{40,72},{48,80},{56,88},{64,... | collective-permute-start | bytes 2949128 | tf_op jit(solution)/shard_map/ppermute | solution.py:468
  570.1 17.6 %collective-permute-start.42 = (f32[384,640]{1,0:T(8,128)S(1)}, f32[384,640]{1,0:T(8,128)S(1)}, u32[]{:S(2)}, u32[]{:S(2)}) collective-permute-start(f32[384,640]{1,0:T(8,128)S(1)} %slice.82), channel_id=1, source_target_pairs={{0,24},{8,0},{16,8},{24,16},{32,56},{40,32},{48,40},{56,48},{64,88... | collective-permute-start | bytes 2949128 | tf_op jit(solution)/shard_map/ppermute | solution.py:468
  573.0 23.6 %collective-permute-start.36 = (f32[512,640]{1,0:T(8,128)S(1)}, f32[512,640]{1,0:T(8,128)S(1)}, u32[]{:S(2)}, u32[]{:S(2)}) collective-permute-start(f32[512,640]{1,0:T(8,128)S(1)} %slice.76), channel_id=1, source_target_pairs={{0,8},{8,16},{16,24},{24,0},{32,40},{40,48},{48,56},{56,32},{64,72... | collective-permute-start | bytes 3932168 | tf_op jit(solution)/shard_map/ppermute | solution.py:468
  584.1 18.8 %collective-permute-start.37 = (f32[512,640]{1,0:T(8,128)S(1)}, f32[512,640]{1,0:T(8,128)S(1)}, u32[]{:S(2)}, u32[]{:S(2)}) collective-permute-start(f32[512,640]{1,0:T(8,128)S(1)} %slice.77), channel_id=1, source_target_pairs={{0,32},{8,40},{16,48},{24,56},{32,64},{40,72},{48,80},{56,88},{64,... | collective-permute-start | bytes 3932168 | tf_op jit(solution)/shard_map/ppermute | solution.py:468
  587.8 18.8 %collective-permute-start.38 = (f32[512,640]{1,0:T(8,128)S(1)}, f32[512,640]{1,0:T(8,128)S(1)}, u32[]{:S(2)}, u32[]{:S(2)}) collective-permute-start(f32[512,640]{1,0:T(8,128)S(1)} %slice.78), channel_id=1, source_target_pairs={{0,24},{8,0},{16,8},{24,16},{32,56},{40,32},{48,40},{56,48},{64,88... | collective-permute-start | bytes 3932168 | tf_op jit(solution)/shard_map/ppermute | solution.py:468
  591.5 20.0 %collective-permute-start.39 = (f32[512,640]{1,0:T(8,128)S(1)}, f32[512,640]{1,0:T(8,128)S(1)}, u32[]{:S(2)}, u32[]{:S(2)}) collective-permute-start(f32[512,640]{1,0:T(8,128)S(1)} %slice.79), channel_id=1, source_target_pairs={{0,96},{8,104},{16,112},{24,120},{32,0},{40,8},{48,16},{56,24},{64... | collective-permute-start | bytes 3932168 | tf_op jit(solution)/shard_map/ppermute | solution.py:468
  592.5 39.3 %collective-permute-start.43 = (f32[384,640]{1,0:T(8,128)}, f32[384,640]{1,0:T(8,128)}, u32[]{:S(2)}, u32[]{:S(2)}) collective-permute-start(f32[384,640]{1,0:T(8,128)} %slice.83), channel_id=1, source_target_pairs={{0,96},{8,104},{16,112},{24,120},{32,0},{40,8},{48,16},{56,24},{64... | collective-permute-start | bytes 2949128 | tf_op jit(solution)/shard_map/ppermute | solution.py:468
  596.7 38.9 %collective-permute-start.44 = (f32[128,640]{1,0:T(8,128)}, f32[128,640]{1,0:T(8,128)}, u32[]{:S(2)}, u32[]{:S(2)}) collective-permute-start(f32[128,640]{1,0:T(8,128)} %slice.84), channel_id=1, source_target_pairs={{0,8},{8,16},{16,24},{24,0},{32,40},{40,48},{48,56},{56,32},{64,72... | collective-permute-start | bytes 983048 | tf_op jit(solution)/shard_map/ppermute | solution.py:468
  604.0 31.6 %collective-permute-start.45 = (f32[128,640]{1,0:T(8,128)}, f32[128,640]{1,0:T(8,128)}, u32[]{:S(2)}, u32[]{:S(2)}) collective-permute-start(f32[128,640]{1,0:T(8,128)} %slice.85), channel_id=1, source_target_pairs={{0,32},{8,40},{16,48},{24,56},{32,64},{40,72},{48,80},{56,88},{64,... | collective-permute-start | bytes 983048 | tf_op jit(solution)/shard_map/ppermute | solution.py:468
  607.7 27.8 %collective-permute-start.46 = (f32[128,640]{1,0:T(8,128)}, f32[128,640]{1,0:T(8,128)}, u32[]{:S(2)}, u32[]{:S(2)}) collective-permute-start(f32[128,640]{1,0:T(8,128)} %slice.86), channel_id=1, source_target_pairs={{0,24},{8,0},{16,8},{24,16},{32,56},{40,32},{48,40},{56,48},{64,88... | collective-permute-start | bytes 983048 | tf_op jit(solution)/shard_map/ppermute | solution.py:468
  612.5 23.0 %collective-permute-start.47 = (f32[128,640]{1,0:T(8,128)}, f32[128,640]{1,0:T(8,128)}, u32[]{:S(2)}, u32[]{:S(2)}) collective-permute-start(f32[128,640]{1,0:T(8,128)} %slice.87), channel_id=1, source_target_pairs={{0,96},{8,104},{16,112},{24,120},{32,0},{40,8},{48,16},{56,24},{64... | collective-permute-start | bytes 983048 | tf_op jit(solution)/shard_map/ppermute | solution.py:468
  (22 other events, 190.9 us)

commit v2 on v1

--- a/solution.py
+++ b/solution.py
@@ -53,7 +53,7 @@
 
 
 def waves(j, level):
-    return (None,) if (j, level) in MIDDLE and level < 2 else (0, 1)
+    return (None,) if (j, level) in MIDDLE else (0, 1)
 
 
 def grad_block(at, tea_ref, x_ref, tab_rows, coef_ref, z_buf, g_buf, out_ref, block):
@@ -84,7 +84,7 @@
     tiles = vocab // sub
     depth = 2 * per
     ring = N_DP // 2
-    few_first = 3
+    few_first, before_lines = 2, 9
 
     def kern(hid_hbm, gain_hbm, mask_hbm, tea_ref, tab_ref, got_late, blocks_ref, x_out, tab_out, coef_ref, all_ref, gh_ref, gg_ref,
              hid_ref, gain_ref, mask_in, w_ref, raw, sends, stage, got_soon, g_buf, t_acc, c_acc, tabs, n_buf, x_buf, inv_buf, square, pay, pay_got, mask_own, mask_got, x_got, tp_got, own_col,
@@ -180,19 +180,21 @@
             rows = slice(None) if w is None else pl.ds(w * late, late)
             src = stage.at[MIDDLE.index((j, level - 1)), :, rows] if level else sends.at[aligned(at[dz, dy] * tokens + kind * half, half, half), rows]
             dst = stage.at[MIDDLE.index((j, level)), :, rows] if (j, level) in MIDDLE else gots[w].at[dz * SIDE + dy, tok]
-            into = (level if w is None else level + w) if (j, level) in MIDDLE else SIDE + w
+            into = level if (j, level) in MIDDLE else SIDE + w
             return remote(src, dst, hop_out.at[min(level, 1)], hop_in.at[into], at[PATHS[j][level]], col)
 
-        def came(level, w=None):
+        def came(level):
             n = sum(at == level for _, at in MIDDLE)
-            rows = slice(None) if w is None else pl.ds(0, late)
-            whole(stage.at[pl.ds(0, n), :, rows], hop_in.at[level + (w or 0)])
+            whole(stage.at[pl.ds(0, n)], hop_in.at[level])
 
         def onward(level, far, *ws):
             for w in ws:
                 for j, at in MIDDLE:
                     if at == level - 1 and far == (len(PATHS[j]) > 2):
-                        hop(j, level, w).start()
+                        if (j, level) not in MIDDLE:
+                            hop(j, level, w).start()
+                        elif w != 1:
+                            hop(j, level, None).start()
 
         def issue(k):
             for j, (_, to) in enumerate(JOBS):
@@ -217,13 +219,16 @@
         square[0:1, 0:tokens] = mask_in[...]
         mask_own[...] = square[0:few]
         mask_col = jnp.transpose(square[...])[0:tokens, 0:1]
-        pay_sent, pay_came = to_dp(pay, pay_got, 0)
-        pay_got[me] = pay[...]
+        my_z, my_y = lax.div(me, SIDE), lax.rem(me, SIDE)
+        for d in range(1, SIDE):
+            remote(pay, pay_got.at[my_z, my_y], dp_sem.at[0, 0], dp_sem.at[0, 1], at[d, 0], col).start()
+        pay_got[my_z, my_y] = pay[...]
         mask_sent, mask_came = to_dp(mask_own, mask_got, 1, pl.ds(0, 1))
         mask_got[me] = mask_own[...]
         for k in range(few_first, N_DP):
             weigh(k)
-            issue(k)
+            if k < before_lines:
+                issue(k)
 
         def keep(r, _):
             here, there = aligned(me * tokens + r * pack, pack, pack), aligned(r * pack, pack, pack)
@@ -259,7 +264,14 @@
             return s_sum, k_sum
 
         zero = jnp.zeros((tokens, LANES), F32)
-        s_sum, k_sum = lax.fori_loop(0, N_DP, forward, (zero, zero))
+        s_sum, k_sum = lax.fori_loop(0, SIDE, forward, (zero, zero))
+        whole(pay_got.at[0, pl.ds(0, SIDE - 1)], dp_sem.at[0, 1])
+        mine = pay_got.at[:, my_y]
+        for d in range(1, SIDE):
+            remote(mine, mine, dp_sem.at[SIDE, 0], dp_sem.at[SIDE, 1], at[0, d], col).start()
+        for k in range(before_lines, N_DP):
+            issue(k)
+        s_sum, k_sum = lax.fori_loop(SIDE, N_DP, forward, (s_sum, k_sum))
         lane = lax.broadcasted_iota(jnp.int32, (tokens, LANES), 1)
         sums = jnp.where(lane == 0, jnp.sum(s_sum, axis=1, keepdims=True), 0.0)
         sums = jnp.where(lane == 1, jnp.sum(t_acc[...], axis=1, keepdims=True), sums)
@@ -275,7 +287,8 @@
         all_ref[me] = line
         dp_sent, dp_came = to_dp(own_row, all_ref, 2, pl.ds(0, SIDE))
         twin = col + 1 - 2 * lax.rem(col, 2)
-        pay_came()
+        lines = pay_got.at[pl.ds(0, SIDE - 1)]
+        whole(lines, dp_sem.at[SIDE, 1])
         mask_came()
         x_got[col] = pay_got[...]
 
@@ -329,13 +342,13 @@
         gn_got[me, 0:1] = line
         gn_sent, gn_came = to_dp(gn_own, gn_got, DOWN, pl.ds(0, 1))
 
-        came(2, 0)
-        onward(DOWN, True, 0)
+        came(2)
+        onward(DOWN, True, 0, 1)
         onward(2, True, 1)
         whole(x_got.at[pl.ds(0, SIDE)], tp_sem.at[SIDE, 1])
 
         def widen(d, _):
-            rows = jnp.concatenate([x_got[j, d] for j in range(N_TP)], axis=0)
+            rows = jnp.concatenate([x_got[j, lax.div(d, SIDE), lax.rem(d, SIDE)] for j in range(N_TP)], axis=0)
             x_out[aligned(d * tokens, tokens, tokens)] = (rows * w_ref[...]).astype(BF16)
             return 0
 
@@ -356,11 +369,6 @@
         whole(sends.at[pl.ds(0, len(JOBS) * half)], hop_out.at[0])
 
         def block(b, _):
-            @pl.when(b == 1)
-            def _():
-                came(2, 1)
-                onward(DOWN, True, 1)
-
             grad_block(at, got_soon, x_out, tab_out[aligned(b * sub, sub)], coef_ref, sends, g_buf, blocks_ref, b)
             return 0
 
@@ -369,8 +377,10 @@
         gg_ref[...] = added(gn_got, slice(1))
         whole(got_late.at[pl.ds(0, N_DP - 1)], hop_in.at[SIDE + 1])
         whole(stage, hop_out.at[1])
-        for ref, sem in (*pay_sent, *mask_sent, *tp_sent, *dp_sent, *rs_sent, *ag_sent, *gn_sent):
+        for ref, sem in (*mask_sent, *tp_sent, *dp_sent, *rs_sent, *ag_sent, *gn_sent):
             whole(ref, sem)
+        whole(pay_got.at[0, pl.ds(0, SIDE - 1)], dp_sem.at[0, 0])
+        whole(lines, dp_sem.at[SIDE, 0])
         whole(x_got.at[pl.ds(0, SIDE - 1)], tp_sem.at[1, 0])
         whole(x_got.at[pl.ds(0, SIDE)], tp_sem.at[SIDE, 0])
 
@@ -386,10 +396,10 @@
             (wide, BF16), ((dim // LANES, LANES), F32), ((1, tokens), F32), ((1, dim), F32), ((ring * tokens, part), BF16), ((N_DP * tokens, part), F32),
             ((len(MIDDLE), half, part), F32), ((N_DP, tokens, part // 2), F32), ((N_DP * tokens, sub), BF16), ((tokens, LANES), F32), ((tokens, LANES), F32),
             ((depth, sub, dim), BF16), (wide, F32), (wide, BF16), ((tokens, LANES), F32), ((LANES, LANES), F32), ((few, dim), F32),
-            ((N_DP, few, dim), F32), (flat, F32), ((N_DP, *flat), F32), ((N_TP, N_DP, few, dim), F32), ((N_TP, tokens, LANES), F32),
+            ((SIDE, SIDE, few, dim), F32), (flat, F32), ((N_DP, *flat), F32), ((N_TP, SIDE, SIDE, few, dim), F32), ((N_TP, tokens, LANES), F32),
             ((tokens, LANES), F32), (flat, F32), ((LANES, LANES), F32), (wide, F32), ((N_TP, few, dim), F32), ((2 * few, dim), F32),
             ((N_TP, 2 * few, dim), F32), ((few, dim), F32), ((N_DP, few, dim), F32))] + [
-            dma((ring,)), dma((depth,)), dma((5,)), dma((2,)), dma((SIDE + 2,)), dma((SIDE, 2)), dma((SIDE + 1, 2))],
+            dma((ring,)), dma((depth,)), dma((5,)), dma((2,)), dma((SIDE + 2,)), dma((SIDE + 1, 2)), dma((SIDE + 1, 2))],
         compiler_params=pltpu.CompilerParams(collective_id=0, has_side_effects=True, vmem_limit_bytes=L_FRONT * MIB),
         cost_estimate=pl.CostEstimate(flops=3 * 10 ** 9, bytes_accessed=100 * MIB, transcendentals=0), name='front')(
             *(pltpu.with_memory_space_constraint(a, pltpu.HBM) for a in (hidden, gain_row, mask_row, teacher, table)))

time: 640 us -> 627 us (0.980)
  waiting for transfers between devices: 373 us -> 346 us
  starting transfers between devices: 56.8 us -> 69.4 us
    ppermute x48, waiting for transfers between devices: 373 us -> 346 us  [send(): lax.ppermute(pair[k], 'dp', [(d, shift(d, dz, dy)) for d in range(N_DP)])]
    ppermute x48, starting transfers between devices: 56.8 us -> 69.4 us  [send(): lax.ppermute(pair[k], 'dp', [(d, shift(d, dz, dy)) for d in range(N_DP)])]
where the time goes in v2:
time: 627 us; the launch traced here: 626 us
  waiting for transfers between devices  346 us (55%)
  Pallas kernels  185 us (30%)
  starting transfers between devices  69.4 us (11%)
  local copies, waits for them, and re-layouts  19.3 us (3%)
    ppermute x48, waiting for transfers between devices, send(): lax.ppermute(pair[k], 'dp', [(d, shift(d, dz, dy)) for d in range(N_DP)])  346 us
    pallas_call x1, Pallas kernels, front(): pl.pallas_call(kern, out_shape=tuple((jax.ShapeDtypeStruct(shape, kind) f...  107 us
    pallas_call x18, Pallas kernels, place(): pl.pallas_call(kern, out_shape=jax.ShapeDtypeStruct((vocab, dim), F32), i...  70.5 us
    ppermute x48, starting transfers between devices, send(): lax.ppermute(pair[k], 'dp', [(d, shift(d, dz, dy)) for d in range(N_DP)])  69.4 us
  transfers between devices with their start and end apart: 48, of which 18 were waited for; matrix products, arithmetic and copies ran while one was open for 2% of the time, Pallas kernels for 12%

profile of v2, /device:TPU:0, one launch (start us, length us, event | category | flops | bytes accessed | tf_op | source)
XLA Modules:
  0.0 625.7 jit_solution(13671812711477490122)
XLA Ops:
  0.6 106.8 %front.1 = (f32[16,64,1024]{2,1,0:T(8,128)S(1)}, f32[2,512,640]{2,1,0:T(8,128)S(1)}, bf16[1024,640]{1,0:T(8,128)(2,1)S(1)}, bf16[2048,640]{1,0:T(8,128)(2,1)S(1)...) custom-call(bf16[64,640]{1,0:T(8,128)(2,1)} %hid_hbm.1, ...), custom_call_target="tpu_custom_call" | custom-call | flops 3000000000 | bytes 104857600 | tf_op jit(solution)/shard_map/front/pallas_call | solution.py:389
  109.2 2.5 collective-permute-start.2
  111.8 2.4 collective-permute-start.3
  114.2 7.2 %finish.1 = f32[2,512,640]{2,1,0:T(8,128)S(1)} custom-call(f32[16,64,1024]{2,1,0:T(8,128)S(1)} %get-tuple-element.84.tea_ref, bf16[1024,640]{1,0:T(8,128)(2,1)S(1)} %get-tuple-element.85.x_ref, bf16[2048,640]{1,0:T(8,128)(2,1)S(1)} %get-tuple-element.86.tab_ref, f32[128,128]{1,0:T(8,128)S(1)} %get-tuple-element.87.coef_ref), custom_call_target="tpu_custom_call" | custom-call | flops 1000000000 | bytes 8388608 | tf_op jit(solution)/shard_map/finish/pallas_call | solution.py:422
  121.7 18.9 %collective-permute-done.refs_0_ = f32[512,640]{1,0:T(8,128)S(1)} collective-permute-done((f32[512,640]{1,0:T(8,128)S(1)}, f32[512,640]{1,0:T(8,128)S(1)}, u32[]{:S(2)}, u32[]{:S(2)}) %collective-permute-start) | collective-permute-done | bytes 1310752 | tf_op jit(solution)/shard_map/ppermute | solution.py:478
  144.5 24.1 %collective-permute-done.4.refs_0_ = f32[512,640]{1,0:T(8,128)S(1)} collective-permute-done((f32[512,640]{1,0:T(8,128)S(1)}, f32[512,640]{1,0:T(8,128)S(1)}, u32[]{:S(2)}, u32[]{:S(2)}) %collective-permute-start.4) | collective-permute-done | bytes 1310752 | tf_op jit(solution)/shard_map/ppermute | solution.py:478
  170.9 2.5 collective-permute-done.5.refs_1_
  175.8 4.1 place.18.refs_4_
  179.9 66.6 %collective-permute-done.7.refs_3_ = f32[512,640]{1,0:T(8,128)S(1)} collective-permute-done((f32[512,640]{1,0:T(8,128)S(1)}, f32[512,640]{1,0:T(8,128)S(1)}, u32[]{:S(2)}, u32[]{:S(2)}) %collective-permute-start.7) | collective-permute-done | bytes 1310752 | tf_op jit(solution)/shard_map/ppermute | solution.py:478
  247.9 4.1 place.19.refs_4_
  260.7 18.6 %collective-permute-done.12.refs_0_ = f32[512,640]{1,0:T(8,128)S(1)} collective-permute-done((f32[512,640]{1,0:T(8,128)S(1)}, f32[512,640]{1,0:T(8,128)S(1)}, u32[]{:S(2)}, u32[]{:S(2)}) %collective-permute-start.12) | collective-permute-done | bytes 1310752 | tf_op jit(solution)/shard_map/ppermute | solution.py:478
  279.3 3.7 collective-permute-start.18
  286.1 3.2 collective-permute-start.19
  289.3 4.1 place.20.refs_2_
  293.8 4.1 place.21.refs_2_
  297.9 4.1 place.22.refs_4_
  302.1 62.4 %collective-permute-done.15.refs_3_ = f32[512,640]{1,0:T(8,128)} collective-permute-done((f32[512,640]{1,0:T(8,128)S(1)}, f32[512,640]{1,0:T(8,128)}, u32[]{:S(2)}, u32[]{:S(2)}) %collective-permute-start.15) | collective-permute-done | bytes 1310752 | tf_op jit(solution)/shard_map/ppermute | solution.py:478
  364.5 3.8 collective-permute-start.24
  369.4 3.2 collective-permute-start.26
  373.0 20.6 %collective-permute-done.24.refs_0_ = f32[512,640]{1,0:T(8,128)S(1)} collective-permute-done((f32[512,640]{1,0:T(8,128)S(1)}, f32[512,640]{1,0:T(8,128)S(1)}, u32[]{:S(2)}, u32[]{:S(2)}) %collective-permute-start.24) | collective-permute-done | bytes 1310752 | tf_op jit(solution)/shard_map/ppermute | solution.py:478
  393.8 28.0 %collective-permute-done.26.refs_2_ = f32[512,640]{1,0:T(8,128)S(1)} collective-permute-done((f32[512,640]{1,0:T(8,128)}, f32[512,640]{1,0:T(8,128)S(1)}, u32[]{:S(2)}, u32[]{:S(2)}) %collective-permute-start.26) | collective-permute-done | bytes 1310752 | tf_op jit(solution)/shard_map/ppermute | solution.py:478
  421.8 3.6 collective-permute-start.22
  427.4 16.1 %collective-permute-done.30.refs_0_ = f32[512,640]{1,0:T(8,128)S(1)} collective-permute-done((f32[512,640]{1,0:T(8,128)S(1)}, f32[512,640]{1,0:T(8,128)S(1)}, u32[]{:S(2)}, u32[]{:S(2)}) %collective-permute-start.30) | collective-permute-done | bytes 1310752 | tf_op jit(solution)/shard_map/ppermute | solution.py:478
  444.7 5.1 collective-permute-start.29
  449.7 4.2 place.23.refs_2_
  454.6 3.6 collective-permute-start.34
  458.2 24.4 %collective-permute-done.22.refs_0_ = f32[1024,640]{1,0:T(8,128)S(1)} collective-permute-done((f32[1024,640]{1,0:T(8,128)S(1)}, f32[1024,640]{1,0:T(8,128)S(1)}, u32[]{:S(2)}, u32[]{:S(2)}) %collective-permute-start.22) | collective-permute-done | bytes 2621472 | tf_op jit(solution)/shard_map/ppermute | solution.py:478
  482.6 14.1 %collective-permute-done.28.refs_0_ = f32[1024,640]{1,0:T(8,128)S(1)} collective-permute-done((f32[1024,640]{1,0:T(8,128)S(1)}, f32[1024,640]{1,0:T(8,128)S(1)}, u32[]{:S(2)}, u32[]{:S(2)}) %collective-permute-start.28) | collective-permute-done | bytes 2621472 | tf_op jit(solution)/shard_map/ppermute | solution.py:478
  496.7 3.3 collective-permute-start.33
  500.0 10.7 %collective-permute-done.29.refs_1_ = f32[1024,640]{1,0:T(8,128)S(1)} collective-permute-done((f32[1024,640]{1,0:T(8,128)S(1)}, f32[1024,640]{1,0:T(8,128)S(1)}, u32[]{:S(2)}, u32[]{:S(2)}) %collective-permute-start.29) | collective-permute-done | bytes 2621472 | tf_op jit(solution)/shard_map/ppermute | solution.py:478
  512.2 4.1 place.24.refs_2_
  516.4 4.6 place.25.refs_2_
  521.0 4.1 place.26.refs_2_
  525.2 4.1 place.27.refs_4_
  530.7 4.1 place.28.refs_2_
  534.8 4.1 place.29.refs_2_
  541.8 17.0 %collective-permute-done.33.refs_1_ = f32[512,640]{1,0:T(8,128)} collective-permute-done((f32[512,640]{1,0:T(8,128)}, f32[512,640]{1,0:T(8,128)}, u32[]{:S(2)}, u32[]{:S(2)}) %collective-permute-start.33) | collective-permute-done | bytes 1310752 | tf_op jit(solution)/shard_map/ppermute | solution.py:478
  558.9 2.5 collective-permute-start.42
  561.8 11.0 %collective-permute-done.41.refs_1_ = f32[384,640]{1,0:T(8,128)S(1)} collective-permute-done((f32[384,640]{1,0:T(8,128)S(1)}, f32[384,640]{1,0:T(8,128)S(1)}, u32[]{:S(2)}, u32[]{:S(2)}) %collective-permute-start.41) | collective-permute-done | bytes 983072 | tf_op jit(solution)/shard_map/ppermute | solution.py:478
  573.9 2.7 collective-permute-start.38
  584.2 7.4 %collective-permute-done.37.refs_1_ = f32[512,640]{1,0:T(8,128)S(1)} collective-permute-done((f32[512,640]{1,0:T(8,128)S(1)}, f32[512,640]{1,0:T(8,128)S(1)}, u32[]{:S(2)}, u32[]{:S(2)}) %collective-permute-start.37) | collective-permute-done | bytes 1310752 | tf_op jit(solution)/shard_map/ppermute | solution.py:478
  593.9 2.8 collective-permute-start.46
  597.7 2.4 collective-permute-start.47
  603.3 3.1 place.30.refs_2_
  606.4 2.6 place.31.refs_2_
  609.1 4.8 place.32.refs_4_
  614.6 4.1 place.33.refs_4_
  618.8 3.7 place.34.refs_4_
  (136 shorter events, 52.4 us)
Async XLA Ops:
  107.7 32.9 %collective-permute-start = (f32[512,640]{1,0:T(8,128)S(1)}, f32[512,640]{1,0:T(8,128)S(1)}, u32[]{:S(2)}, u32[]{:S(2)}) collective-permute-start(f32[512,640]{1,0:T(8,128)S(1)} %get-tuple-element.82.refs_0_), channel_id=1, source_target_pairs={{0,32},{8,40},{16,48},{24,56},{32,64},{40,72},{48,80},{56,88},{64,... | collective-permute-start | bytes 3932168 | tf_op jit(solution)/shard_map/ppermute | solution.py:478
  108.9 32.7 %collective-permute-start.1 = (f32[512,640]{1,0:T(8,128)S(1)}, f32[512,640]{1,0:T(8,128)S(1)}, u32[]{:S(2)}, u32[]{:S(2)}) collective-permute-start(f32[512,640]{1,0:T(8,128)S(1)} %get-tuple-element.83.refs_1_), channel_id=1, source_target_pairs={{0,8},{8,16},{16,24},{24,0},{32,40},{40,48},{48,56},{56,32},{64,72... | collective-permute-start | bytes 3932168 | tf_op jit(solution)/shard_map/ppermute | solution.py:478
  109.2 33.7 %collective-permute-start.2 = (f32[512,640]{1,0:T(8,128)S(1)}, f32[512,640]{1,0:T(8,128)S(1)}, u32[]{:S(2)}, u32[]{:S(2)}) collective-permute-start(f32[512,640]{1,0:T(8,128)S(1)} %get-tuple-element.82.refs_0_), channel_id=1, source_target_pairs={{0,96},{8,104},{16,112},{24,120},{32,0},{40,8},{48,16},{56,24},{64... | collective-permute-start | bytes 3932168 | tf_op jit(solution)/shard_map/ppermute | solution.py:478
  111.8 31.9 %collective-permute-start.3 = (f32[512,640]{1,0:T(8,128)S(1)}, f32[512,640]{1,0:T(8,128)S(1)}, u32[]{:S(2)}, u32[]{:S(2)}) collective-permute-start(f32[512,640]{1,0:T(8,128)S(1)} %get-tuple-element.83.refs_1_), channel_id=1, source_target_pairs={{0,24},{8,0},{16,8},{24,16},{32,56},{40,32},{48,40},{56,48},{64,88... | collective-permute-start | bytes 3932168 | tf_op jit(solution)/shard_map/ppermute | solution.py:478
  121.6 47.1 %collective-permute-start.4 = (f32[512,640]{1,0:T(8,128)S(1)}, f32[512,640]{1,0:T(8,128)S(1)}, u32[]{:S(2)}, u32[]{:S(2)}) collective-permute-start(f32[512,640]{1,0:T(8,128)S(1)} %get-tuple-element.153.refs_2_), channel_id=1, source_target_pairs={{0,32},{8,40},{16,48},{24,56},{32,64},{40,72},{48,80},{56,88},{64,... | collective-permute-start | bytes 3932168 | tf_op jit(solution)/shard_map/ppermute | solution.py:478
  140.6 32.9 %collective-permute-start.5 = (f32[512,640]{1,0:T(8,128)S(1)}, f32[512,640]{1,0:T(8,128)S(1)}, u32[]{:S(2)}, u32[]{:S(2)}) collective-permute-start(f32[512,640]{1,0:T(8,128)S(1)} %get-tuple-element.152.refs_3_), channel_id=1, source_target_pairs={{0,8},{8,16},{16,24},{24,0},{32,40},{40,48},{48,56},{56,32},{64,72... | collective-permute-start | bytes 3932168 | tf_op jit(solution)/shard_map/ppermute | solution.py:478
  141.6 32.8 %collective-permute-start.6 = (f32[512,640]{1,0:T(8,128)S(1)}, f32[512,640]{1,0:T(8,128)S(1)}, u32[]{:S(2)}, u32[]{:S(2)}) collective-permute-start(f32[512,640]{1,0:T(8,128)S(1)} %get-tuple-element.153.refs_2_), channel_id=1, source_target_pairs={{0,96},{8,104},{16,112},{24,120},{32,0},{40,8},{48,16},{56,24},{64... | collective-permute-start | bytes 3932168 | tf_op jit(solution)/shard_map/ppermute | solution.py:478
  143.0 109.0 %collective-permute-start.8 = (f32[1024,640]{1,0:T(8,128)S(1)}, f32[1024,640]{1,0:T(8,128)S(1)}, u32[]{:S(2)}, u32[]{:S(2)}) collective-permute-start(f32[1024,640]{1,0:T(8,128)S(1)} %pad_maximum_fusion), channel_id=1, source_target_pairs={{0,8},{8,16},{16,24},{24,0},{32,40},{40,48},{48,56},{56,32},{64,72... | collective-permute-start | bytes 7864328 | tf_op jit(solution)/shard_map/ppermute | solution.py:478
  143.7 108.4 %collective-permute-start.9 = (f32[1024,640]{1,0:T(8,128)S(1)}, f32[1024,640]{1,0:T(8,128)S(1)}, u32[]{:S(2)}, u32[]{:S(2)}) collective-permute-start(f32[1024,640]{1,0:T(8,128)S(1)} %pad_maximum_fusion.1), channel_id=1, source_target_pairs={{0,32},{8,40},{16,48},{24,56},{32,64},{40,72},{48,80},{56,88},{64,... | collective-permute-start | bytes 7864328 | tf_op jit(solution)/shard_map/ppermute | solution.py:478
  168.7 87.6 %collective-permute-start.10 = (f32[1024,640]{1,0:T(8,128)S(1)}, f32[1024,640]{1,0:T(8,128)S(1)}, u32[]{:S(2)}, u32[]{:S(2)}) collective-permute-start(f32[1024,640]{1,0:T(8,128)S(1)} %pad_maximum_fusion), channel_id=1, source_target_pairs={{0,24},{8,0},{16,8},{24,16},{32,56},{40,32},{48,40},{56,48},{64,88... | collective-permute-start | bytes 7864328 | tf_op jit(solution)/shard_map/ppermute | solution.py:478
  173.4 87.3 %collective-permute-start.11 = (f32[1024,640]{1,0:T(8,128)S(1)}, f32[1024,640]{1,0:T(8,128)S(1)}, u32[]{:S(2)}, u32[]{:S(2)}) collective-permute-start(f32[1024,640]{1,0:T(8,128)S(1)} %pad_maximum_fusion.1), channel_id=1, source_target_pairs={{0,96},{8,104},{16,112},{24,120},{32,0},{40,8},{48,16},{56,24},{64... | collective-permute-start | bytes 7864328 | tf_op jit(solution)/shard_map/ppermute | solution.py:478
  174.4 72.0 %collective-permute-start.7 = (f32[512,640]{1,0:T(8,128)S(1)}, f32[512,640]{1,0:T(8,128)S(1)}, u32[]{:S(2)}, u32[]{:S(2)}) collective-permute-start(f32[512,640]{1,0:T(8,128)S(1)} %get-tuple-element.152.refs_3_), channel_id=1, source_target_pairs={{0,24},{8,0},{16,8},{24,16},{32,56},{40,32},{48,40},{56,48},{64,88... | collective-permute-start | bytes 3932168 | tf_op jit(solution)/shard_map/ppermute | solution.py:478
  246.4 32.9 %collective-permute-start.12 = (f32[512,640]{1,0:T(8,128)S(1)}, f32[512,640]{1,0:T(8,128)S(1)}, u32[]{:S(2)}, u32[]{:S(2)}) collective-permute-start(f32[512,640]{1,0:T(8,128)S(1)} %collective-permute-done.refs_0_), channel_id=1, source_target_pairs={{0,32},{8,40},{16,48},{24,56},{32,64},{40,72},{48,80},{56,88},{64,... | collective-permute-start | bytes 3932168 | tf_op jit(solution)/shard_map/ppermute | solution.py:478
  252.0 33.0 %collective-permute-start.13 = (f32[512,640]{1,0:T(8,128)S(1)}, f32[512,640]{1,0:T(8,128)}, u32[]{:S(2)}, u32[]{:S(2)}) collective-permute-start(f32[512,640]{1,0:T(8,128)S(1)} %collective-permute-done.1.refs_1_), channel_id=1, source_target_pairs={{0,8},{8,16},{16,24},{24,0},{32,40},{40,48},{48,56},{56,32},{64,72... | collective-permute-start | bytes 3932168 | tf_op jit(solution)/shard_map/ppermute | solution.py:478
  252.1 34.0 %collective-permute-start.14 = (f32[512,640]{1,0:T(8,128)S(1)}, f32[512,640]{1,0:T(8,128)}, u32[]{:S(2)}, u32[]{:S(2)}) collective-permute-start(f32[512,640]{1,0:T(8,128)S(1)} %collective-permute-done.6.refs_2_), channel_id=1, source_target_pairs={{0,96},{8,104},{16,112},{24,120},{32,0},{40,8},{48,16},{56,24},{64... | collective-permute-start | bytes 3932168 | tf_op jit(solution)/shard_map/ppermute | solution.py:478
  256.3 112.0 %collective-permute-start.16 = (f32[1024,640]{1,0:T(8,128)}, f32[1024,640]{1,0:T(8,128)S(1)}, u32[]{:S(2)}, u32[]{:S(2)}) collective-permute-start(f32[1024,640]{1,0:T(8,128)} %constant_dynamic-update-slice_fusion), channel_id=1, source_target_pairs={{0,8},{8,16},{16,24},{24,0},{32,40},{40,48},{48,56},{56,32},{64,72... | collective-permute-start | bytes 7864328 | tf_op jit(solution)/shard_map/ppermute | solution.py:478
  260.7 107.6 %collective-permute-start.17 = (f32[1024,640]{1,0:T(8,128)}, f32[1024,640]{1,0:T(8,128)S(1)}, u32[]{:S(2)}, u32[]{:S(2)}) collective-permute-start(f32[1024,640]{1,0:T(8,128)} %constant_dynamic-update-slice_fusion.2), channel_id=1, source_target_pairs={{0,32},{8,40},{16,48},{24,56},{32,64},{40,72},{48,80},{56,88},{64,... | collective-permute-start | bytes 7864328 | tf_op jit(solution)/shard_map/ppermute | solution.py:478
  279.3 90.1 %collective-permute-start.18 = (f32[1024,640]{1,0:T(8,128)}, f32[1024,640]{1,0:T(8,128)}, u32[]{:S(2)}, u32[]{:S(2)}) collective-permute-start(f32[1024,640]{1,0:T(8,128)} %constant_dynamic-update-slice_fusion), channel_id=1, source_target_pairs={{0,24},{8,0},{16,8},{24,16},{32,56},{40,32},{48,40},{56,48},{64,88... | collective-permute-start | bytes 7864328 | tf_op jit(solution)/shard_map/ppermute | solution.py:478
  285.0 79.5 %collective-permute-start.15 = (f32[512,640]{1,0:T(8,128)S(1)}, f32[512,640]{1,0:T(8,128)}, u32[]{:S(2)}, u32[]{:S(2)}) collective-permute-start(f32[512,640]{1,0:T(8,128)S(1)} %collective-permute-done.7.refs_3_), channel_id=1, source_target_pairs={{0,24},{8,0},{16,8},{24,16},{32,56},{40,32},{48,40},{56,48},{64,88... | collective-permute-start | bytes 3932168 | tf_op jit(solution)/shard_map/ppermute | solution.py:478
  286.1 86.5 %collective-permute-start.19 = (f32[1024,640]{1,0:T(8,128)}, f32[1024,640]{1,0:T(8,128)}, u32[]{:S(2)}, u32[]{:S(2)}) collective-permute-start(f32[1024,640]{1,0:T(8,128)} %constant_dynamic-update-slice_fusion.2), channel_id=1, source_target_pairs={{0,96},{8,104},{16,112},{24,120},{32,0},{40,8},{48,16},{56,24},{64... | collective-permute-start | bytes 7864328 | tf_op jit(solution)/shard_map/ppermute | solution.py:478
  364.5 29.0 %collective-permute-start.24 = (f32[512,640]{1,0:T(8,128)S(1)}, f32[512,640]{1,0:T(8,128)S(1)}, u32[]{:S(2)}, u32[]{:S(2)}) collective-permute-start(f32[512,640]{1,0:T(8,128)S(1)} %collective-permute-done.12.refs_0_), channel_id=1, source_target_pairs={{0,24},{8,0},{16,8},{24,16},{32,56},{40,32},{48,40},{56,48},{64,88... | collective-permute-start | bytes 3932168 | tf_op jit(solution)/shard_map/ppermute | solution.py:478
  368.3 75.3 %collective-permute-start.20 = (f32[1024,640]{1,0:T(8,128)S(1)}, f32[1024,640]{1,0:T(8,128)S(1)}, u32[]{:S(2)}, u32[]{:S(2)}) collective-permute-start(f32[1024,640]{1,0:T(8,128)S(1)} %get-tuple-element.113), channel_id=1, source_target_pairs={{0,8},{8,16},{16,24},{24,0},{32,40},{40,48},{48,56},{56,32},{64,72... | collective-permute-start | bytes 7864328 | tf_op jit(solution)/shard_map/ppermute | solution.py:478
  368.3 25.3 %collective-permute-start.25 = (f32[512,640]{1,0:T(8,128)}, f32[512,640]{1,0:T(8,128)S(1)}, u32[]{:S(2)}, u32[]{:S(2)}) collective-permute-start(f32[512,640]{1,0:T(8,128)} %collective-permute-done.13.refs_1_), channel_id=1, source_target_pairs={{0,96},{8,104},{16,112},{24,120},{32,0},{40,8},{48,16},{56,24},{64... | collective-permute-start | bytes 3932168 | tf_op jit(solution)/shard_map/ppermute | solution.py:478
  369.4 52.3 %collective-permute-start.26 = (f32[512,640]{1,0:T(8,128)}, f32[512,640]{1,0:T(8,128)S(1)}, u32[]{:S(2)}, u32[]{:S(2)}) collective-permute-start(f32[512,640]{1,0:T(8,128)} %collective-permute-done.14.refs_2_), channel_id=1, source_target_pairs={{0,24},{8,0},{16,8},{24,16},{32,56},{40,32},{48,40},{56,48},{64,88... | collective-permute-start | bytes 3932168 | tf_op jit(solution)/shard_map/ppermute | solution.py:478
  372.6 52.8 %collective-permute-start.27 = (f32[512,640]{1,0:T(8,128)}, f32[512,640]{1,0:T(8,128)S(1)}, u32[]{:S(2)}, u32[]{:S(2)}) collective-permute-start(f32[512,640]{1,0:T(8,128)} %collective-permute-done.15.refs_3_), channel_id=1, source_target_pairs={{0,96},{8,104},{16,112},{24,120},{32,0},{40,8},{48,16},{56,24},{64... | collective-permute-start | bytes 3932168 | tf_op jit(solution)/shard_map/ppermute | solution.py:478
  393.6 49.9 %collective-permute-start.30 = (f32[512,640]{1,0:T(8,128)S(1)}, f32[512,640]{1,0:T(8,128)S(1)}, u32[]{:S(2)}, u32[]{:S(2)}) collective-permute-start(f32[512,640]{1,0:T(8,128)S(1)} %collective-permute-done.12.refs_0_), channel_id=1, source_target_pairs={{0,8},{8,16},{16,24},{24,0},{32,40},{40,48},{48,56},{56,32},{64,72... | collective-permute-start | bytes 3932168 | tf_op jit(solution)/shard_map/ppermute | solution.py:478
  393.6 60.9 %collective-permute-start.21 = (f32[1024,640]{1,0:T(8,128)S(1)}, f32[1024,640]{1,0:T(8,128)S(1)}, u32[]{:S(2)}, u32[]{:S(2)}) collective-permute-start(f32[1024,640]{1,0:T(8,128)S(1)} %get-tuple-element.114), channel_id=1, source_target_pairs={{0,32},{8,40},{16,48},{24,56},{32,64},{40,72},{48,80},{56,88},{64,... | collective-permute-start | bytes 7864328 | tf_op jit(solution)/shard_map/ppermute | solution.py:478
  421.8 60.8 %collective-permute-start.22 = (f32[1024,640]{1,0:T(8,128)S(1)}, f32[1024,640]{1,0:T(8,128)S(1)}, u32[]{:S(2)}, u32[]{:S(2)}) collective-permute-start(f32[1024,640]{1,0:T(8,128)S(1)} %get-tuple-element.113), channel_id=1, source_target_pairs={{0,24},{8,0},{16,8},{24,16},{32,56},{40,32},{48,40},{56,48},{64,88... | collective-permute-start | bytes 7864328 | tf_op jit(solution)/shard_map/ppermute | solution.py:478
  426.4 56.2 %collective-permute-start.23 = (f32[1024,640]{1,0:T(8,128)S(1)}, f32[1024,640]{1,0:T(8,128)S(1)}, u32[]{:S(2)}, u32[]{:S(2)}) collective-permute-start(f32[1024,640]{1,0:T(8,128)S(1)} %get-tuple-element.114), channel_id=1, source_target_pairs={{0,96},{8,104},{16,112},{24,120},{32,0},{40,8},{48,16},{56,24},{64... | collective-permute-start | bytes 7864328 | tf_op jit(solution)/shard_map/ppermute | solution.py:478
  443.5 53.2 %collective-permute-start.28 = (f32[1024,640]{1,0:T(8,128)S(1)}, f32[1024,640]{1,0:T(8,128)S(1)}, u32[]{:S(2)}, u32[]{:S(2)}) collective-permute-start(f32[1024,640]{1,0:T(8,128)S(1)} %collective-permute-done.8.refs_0_), channel_id=1, source_target_pairs={{0,8},{8,16},{16,24},{24,0},{32,40},{40,48},{48,56},{56,32},{64,72... | collective-permute-start | bytes 7864328 | tf_op jit(solution)/shard_map/ppermute | solution.py:478
  444.7 66.1 %collective-permute-start.29 = (f32[1024,640]{1,0:T(8,128)S(1)}, f32[1024,640]{1,0:T(8,128)S(1)}, u32[]{:S(2)}, u32[]{:S(2)}) collective-permute-start(f32[1024,640]{1,0:T(8,128)S(1)} %collective-permute-done.9.refs_1_), channel_id=1, source_target_pairs={{0,32},{8,40},{16,48},{24,56},{32,64},{40,72},{48,80},{56,88},{64,... | collective-permute-start | bytes 7864328 | tf_op jit(solution)/shard_map/ppermute | solution.py:478
  454.6 122.1 %collective-permute-start.34 = (f32[1024,640]{1,0:T(8,128)}, f32[1024,640]{1,0:T(8,128)}, u32[]{:S(2)}, u32[]{:S(2)}) collective-permute-start(f32[1024,640]{1,0:T(8,128)} %collective-permute-done.18.refs_0_), channel_id=1, source_target_pairs={{0,24},{8,0},{16,8},{24,16},{32,56},{40,32},{48,40},{56,48},{64,88... | collective-permute-start | bytes 7864328 | tf_op jit(solution)/shard_map/ppermute | solution.py:478
  482.6 56.4 %collective-permute-start.31 = (f32[512,640]{1,0:T(8,128)}, f32[512,640]{1,0:T(8,128)}, u32[]{:S(2)}, u32[]{:S(2)}) collective-permute-start(f32[512,640]{1,0:T(8,128)} %collective-permute-done.13.refs_1_), channel_id=1, source_target_pairs={{0,32},{8,40},{16,48},{24,56},{32,64},{40,72},{48,80},{56,88},{64,... | collective-permute-start | bytes 3932168 | tf_op jit(solution)/shard_map/ppermute | solution.py:478
  482.6 58.8 %collective-permute-start.32 = (f32[512,640]{1,0:T(8,128)}, f32[512,640]{1,0:T(8,128)}, u32[]{:S(2)}, u32[]{:S(2)}) collective-permute-start(f32[512,640]{1,0:T(8,128)} %collective-permute-done.14.refs_2_), channel_id=1, source_target_pairs={{0,8},{8,16},{16,24},{24,0},{32,40},{40,48},{48,56},{56,32},{64,72... | collective-permute-start | bytes 3932168 | tf_op jit(solution)/shard_map/ppermute | solution.py:478
  496.7 62.1 %collective-permute-start.33 = (f32[512,640]{1,0:T(8,128)}, f32[512,640]{1,0:T(8,128)}, u32[]{:S(2)}, u32[]{:S(2)}) collective-permute-start(f32[512,640]{1,0:T(8,128)} %collective-permute-done.15.refs_3_), channel_id=1, source_target_pairs={{0,32},{8,40},{16,48},{24,56},{32,64},{40,72},{48,80},{56,88},{64,... | collective-permute-start | bytes 3932168 | tf_op jit(solution)/shard_map/ppermute | solution.py:478
  510.7 69.1 %collective-permute-start.35 = (f32[1024,640]{1,0:T(8,128)}, f32[1024,640]{1,0:T(8,128)}, u32[]{:S(2)}, u32[]{:S(2)}) collective-permute-start(f32[1024,640]{1,0:T(8,128)} %collective-permute-done.19.refs_1_), channel_id=1, source_target_pairs={{0,96},{8,104},{16,112},{24,120},{32,0},{40,8},{48,16},{56,24},{64... | collective-permute-start | bytes 7864328 | tf_op jit(solution)/shard_map/ppermute | solution.py:478
  539.1 22.6 %collective-permute-start.40 = (f32[384,640]{1,0:T(8,128)S(1)}, f32[384,640]{1,0:T(8,128)S(1)}, u32[]{:S(2)}, u32[]{:S(2)}) collective-permute-start(f32[384,640]{1,0:T(8,128)S(1)} %slice.80), channel_id=1, source_target_pairs={{0,8},{8,16},{16,24},{24,0},{32,40},{40,48},{48,56},{56,32},{64,72... | collective-permute-start | bytes 2949128 | tf_op jit(solution)/shard_map/ppermute | solution.py:478
  541.4 31.4 %collective-permute-start.41 = (f32[384,640]{1,0:T(8,128)S(1)}, f32[384,640]{1,0:T(8,128)S(1)}, u32[]{:S(2)}, u32[]{:S(2)}) collective-permute-start(f32[384,640]{1,0:T(8,128)S(1)} %slice.81), channel_id=1, source_target_pairs={{0,32},{8,40},{16,48},{24,56},{32,64},{40,72},{48,80},{56,88},{64,... | collective-permute-start | bytes 2949128 | tf_op jit(solution)/shard_map/ppermute | solution.py:478
  558.9 15.1 %collective-permute-start.42 = (f32[384,640]{1,0:T(8,128)S(1)}, f32[384,640]{1,0:T(8,128)S(1)}, u32[]{:S(2)}, u32[]{:S(2)}) collective-permute-start(f32[384,640]{1,0:T(8,128)S(1)} %slice.82), channel_id=1, source_target_pairs={{0,24},{8,0},{16,8},{24,16},{32,56},{40,32},{48,40},{56,48},{64,88... | collective-permute-start | bytes 2949128 | tf_op jit(solution)/shard_map/ppermute | solution.py:478
  561.7 22.5 %collective-permute-start.36 = (f32[512,640]{1,0:T(8,128)S(1)}, f32[512,640]{1,0:T(8,128)S(1)}, u32[]{:S(2)}, u32[]{:S(2)}) collective-permute-start(f32[512,640]{1,0:T(8,128)S(1)} %slice.76), channel_id=1, source_target_pairs={{0,8},{8,16},{16,24},{24,0},{32,40},{40,48},{48,56},{56,32},{64,72... | collective-permute-start | bytes 3932168 | tf_op jit(solution)/shard_map/ppermute | solution.py:478
  572.8 18.8 %collective-permute-start.37 = (f32[512,640]{1,0:T(8,128)S(1)}, f32[512,640]{1,0:T(8,128)S(1)}, u32[]{:S(2)}, u32[]{:S(2)}) collective-permute-start(f32[512,640]{1,0:T(8,128)S(1)} %slice.77), channel_id=1, source_target_pairs={{0,32},{8,40},{16,48},{24,56},{32,64},{40,72},{48,80},{56,88},{64,... | collective-permute-start | bytes 3932168 | tf_op jit(solution)/shard_map/ppermute | solution.py:478
  573.9 18.8 %collective-permute-start.38 = (f32[512,640]{1,0:T(8,128)S(1)}, f32[512,640]{1,0:T(8,128)S(1)}, u32[]{:S(2)}, u32[]{:S(2)}) collective-permute-start(f32[512,640]{1,0:T(8,128)S(1)} %slice.78), channel_id=1, source_target_pairs={{0,24},{8,0},{16,8},{24,16},{32,56},{40,32},{48,40},{56,48},{64,88... | collective-permute-start | bytes 3932168 | tf_op jit(solution)/shard_map/ppermute | solution.py:478
  576.6 20.0 %collective-permute-start.39 = (f32[512,640]{1,0:T(8,128)S(1)}, f32[512,640]{1,0:T(8,128)S(1)}, u32[]{:S(2)}, u32[]{:S(2)}) collective-permute-start(f32[512,640]{1,0:T(8,128)S(1)} %slice.79), channel_id=1, source_target_pairs={{0,96},{8,104},{16,112},{24,120},{32,0},{40,8},{48,16},{56,24},{64... | collective-permute-start | bytes 3932168 | tf_op jit(solution)/shard_map/ppermute | solution.py:478
  579.9 38.9 %collective-permute-start.43 = (f32[384,640]{1,0:T(8,128)}, f32[384,640]{1,0:T(8,128)}, u32[]{:S(2)}, u32[]{:S(2)}) collective-permute-start(f32[384,640]{1,0:T(8,128)} %slice.83), channel_id=1, source_target_pairs={{0,96},{8,104},{16,112},{24,120},{32,0},{40,8},{48,16},{56,24},{64... | collective-permute-start | bytes 2949128 | tf_op jit(solution)/shard_map/ppermute | solution.py:478
  584.2 38.3 %collective-permute-start.44 = (f32[128,640]{1,0:T(8,128)}, f32[128,640]{1,0:T(8,128)}, u32[]{:S(2)}, u32[]{:S(2)}) collective-permute-start(f32[128,640]{1,0:T(8,128)} %slice.84), channel_id=1, source_target_pairs={{0,8},{8,16},{16,24},{24,0},{32,40},{40,48},{48,56},{56,32},{64,72... | collective-permute-start | bytes 983048 | tf_op jit(solution)/shard_map/ppermute | solution.py:478
  592.7 29.8 %collective-permute-start.45 = (f32[128,640]{1,0:T(8,128)}, f32[128,640]{1,0:T(8,128)}, u32[]{:S(2)}, u32[]{:S(2)}) collective-permute-start(f32[128,640]{1,0:T(8,128)} %slice.85), channel_id=1, source_target_pairs={{0,32},{8,40},{16,48},{24,56},{32,64},{40,72},{48,80},{56,88},{64,... | collective-permute-start | bytes 983048 | tf_op jit(solution)/shard_map/ppermute | solution.py:478
  593.9 28.6 %collective-permute-start.46 = (f32[128,640]{1,0:T(8,128)}, f32[128,640]{1,0:T(8,128)}, u32[]{:S(2)}, u32[]{:S(2)}) collective-permute-start(f32[128,640]{1,0:T(8,128)} %slice.86), channel_id=1, source_target_pairs={{0,24},{8,0},{16,8},{24,16},{32,56},{40,32},{48,40},{56,48},{64,88... | collective-permute-start | bytes 983048 | tf_op jit(solution)/shard_map/ppermute | solution.py:478
  597.7 24.8 %collective-permute-start.47 = (f32[128,640]{1,0:T(8,128)}, f32[128,640]{1,0:T(8,128)}, u32[]{:S(2)}, u32[]{:S(2)}) collective-permute-start(f32[128,640]{1,0:T(8,128)} %slice.87), channel_id=1, source_target_pairs={{0,96},{8,104},{16,112},{24,120},{32,0},{40,8},{48,16},{56,24},{64... | collective-permute-start | bytes 983048 | tf_op jit(solution)/shard_map/ppermute | solution.py:478
  (22 other events, 186.9 us)
